TPU v7x, 32 devices: a whole 2x2x4 slice. The times are simulated.
32 devices in a mesh: cuts: 4 (over x, core), exp: 2 (over y), fsdp: 4 (over z).
Axes of the slice: x: 2, y: 2, z: 4, core: 2. Of those that a mesh axis runs over, the one named last changes fastest.
Arguments:
- tokens: bfloat16 [4096, 4096], P(('cuts', 'exp', 'fsdp')), may hold values from -6 to 6
- out_grad: bfloat16 [4096, 4096], P(('cuts', 'exp', 'fsdp')), may hold values from -6 to 6
- expert_ids: int32 [4096, 2], P(('cuts', 'exp', 'fsdp')), may hold values from 0 to 7, as said below
- gate_probs: bfloat16 [4096, 2], P(('cuts', 'exp', 'fsdp')), may hold values from 0.049804688 to 0.94921875
- params: float32 [3, 8, 4096, 256], P(None, 'exp', ('cuts', 'fsdp')), may hold values from -0.1875 to 0.1875
- moment_first: float32 [3, 8, 4096, 256], P(None, 'exp', ('cuts', 'fsdp')), may hold values from -60 to 60
- moment_second: float32 [3, 8, 4096, 256], P(None, 'exp', ('cuts', 'fsdp')), may hold values from 64 to 1024
Outputs:
- token_grad: bfloat16 [4096, 4096], P(('cuts', 'exp', 'fsdp'))
- gate_grad: bfloat16 [4096, 2], P(('cuts', 'exp', 'fsdp'))
- new_params: float32 [3, 8, 4096, 256], P(None, 'exp', ('cuts', 'fsdp'))
- new_first: float32 [3, 8, 4096, 256], P(None, 'exp', ('cuts', 'fsdp'))
- new_second: float32 [3, 8, 4096, 256], P(None, 'exp', ('cuts', 'fsdp'))
Inputs may be any that keep to these rules, and one draw needn't show every extreme that they name: `expert_ids`: the two ids of a token differ. Among the tokens of one device no expert is named more than 40 times. Each device names some expert exactly 40 times, and the devices that share their cuts and fsdp indices have one such expert in common.
All inputs are finite; a program needn't handle non-finite values.
Results may differ from a plain program's by a relative error of at most 0.0079.
Values may be sent and summed in bfloat16 or wider, within the bound.
A program may use at most 192 MiB of HBM per device.

v0:
```python
import jax
import jax.numpy as jnp
from jax import lax
from jax.sharding import PartitionSpec as P

EXPERTS = 8


decay_first = 0.9
decay_second = 0.95
correct_first = 1.0 - 0.9**10
correct_second = 1.0 - 0.95**10
epsilon = 1e-08
learn_rate = 0.0003
weight_decay = 0.1
GROUP = ("cuts", "fsdp")


def adam_update(params, gradient, moment_first, moment_second):
    new_first = decay_first * moment_first + (1.0 - decay_first) * gradient
    new_second = decay_second * moment_second + (1.0 - decay_second) * gradient * gradient
    stepped = new_first / correct_first / (jnp.sqrt(new_second / correct_second) + epsilon)
    new_params = params - learn_rate * (stepped + weight_decay * params)
    return (new_params, new_first, new_second)


def per_device(tokens, out_grad, expert_ids, gate_probs, params, moment_first, moment_second):
    token_count, width = tokens.shape
    local = params.shape[1]
    rows = params.shape[2]
    hidden_units = params.shape[3]
    shares = width // rows
    exp_count = lax.axis_size("exp")
    capacity = 10 * token_count // 32
    me = lax.axis_index("exp")
    local_slots = local * capacity

    weights = params.astype(jnp.bfloat16)
    w_in = jnp.concatenate([weights[0], weights[1]], axis=2)
    w_down = weights[2]

    cores = 2
    cuts = lax.axis_size("cuts")
    shards = lax.axis_size("fsdp")
    chips = cuts // cores
    core_groups = [[chip * cores + core for core in range(cores)] for chip in range(chips)]
    chip_groups = [
        [(chip * cores + core) * shards + shard for chip in range(chips) for shard in range(shards)]
        for core in range(cores)
    ]

    def spread(array):
        parts = array.reshape(array.shape[0], shares, rows).transpose(1, 0, 2)
        return parts

    def exchange(parts):
        parts = lax.all_to_all(parts, GROUP, split_axis=0, concat_axis=0, tiled=True)
        return lax.all_gather(parts, "exp", axis=1, tiled=False)

    flat_ids = expert_ids.reshape(-1)
    onehot = (flat_ids[:, None] == jnp.arange(EXPERTS, dtype=jnp.int32)).astype(jnp.int32)
    before = jnp.cumsum(onehot, axis=0) - onehot
    position = jnp.sum(before * onehot, axis=1)
    extra = jnp.concatenate(
        [flat_ids.astype(jnp.bfloat16), position.astype(jnp.bfloat16), gate_probs.reshape(-1)]
    )
    extra_rows = extra.shape[0] // rows
    padded = -(-extra_rows // 8) * 8
    extra = jnp.pad(extra.reshape(extra_rows, rows), ((0, padded - extra_rows), (0, 0)))
    extra = jnp.broadcast_to(extra[None], (shares, padded, rows))

    sources = shares * exp_count
    token_parts = exchange(jnp.concatenate([spread(tokens), extra], axis=1))
    upstream_parts = exchange(spread(out_grad))
    everyone = token_parts[:, :, token_count : token_count + extra_rows, :]
    everyone = everyone.reshape(sources, 3, token_count, 2)
    ids = everyone[:, 0].astype(jnp.int32)
    all_slots = ids * capacity + everyone[:, 1].astype(jnp.int32) - me * local_slots
    all_gates = everyone[:, 2].astype(jnp.float32)
    columns = jnp.arange(local_slots, dtype=jnp.int32)
    place = (all_slots[:, :, :, None] == columns).astype(jnp.bfloat16).sum(axis=2)

    def pick(array):
        array = array[:, :, :token_count].reshape(sources, token_count, rows)
        picked = jnp.einsum("ntc,ntd->ncd", place, array, preferred_element_type=jnp.bfloat16)
        picked = picked.reshape(sources, local, capacity, rows).transpose(1, 0, 2, 3)
        return picked.reshape(local, sources * capacity, rows)

    inputs = pick(token_parts)

    def partial_sums(left, right):
        out = jnp.einsum("esd,edf->esf", left, right, preferred_element_type=jnp.float32)
        out = out.astype(jnp.bfloat16)
        out = out.reshape(local, chips, cores, shards, exp_count * capacity, right.shape[2])
        out = out.transpose(2, 1, 3, 0, 4, 5)
        out = lax.all_to_all(
            out, "cuts", split_axis=0, concat_axis=0, tiled=True, axis_index_groups=core_groups
        )
        return jnp.sum(out.astype(jnp.float32), axis=0).astype(jnp.bfloat16)

    def finish(out):
        out = out.reshape((chips * shards,) + out.shape[2:])
        out = lax.all_to_all(
            out, GROUP, split_axis=0, concat_axis=0, tiled=True, axis_index_groups=chip_groups
        )
        return jnp.sum(out.astype(jnp.float32), axis=0)

    pre = partial_sums(inputs, w_in)
    pre, upstream_parts = lax.optimization_barrier((pre, upstream_parts))
    upstream = pick(upstream_parts)
    projected = finish(partial_sums(upstream, w_down))
    pre = finish(pre)
    pre_gate = pre[:, :, :hidden_units]
    pre_up = pre[:, :, hidden_units:]

    start = lax.axis_index(GROUP) * exp_count
    my_slots = lax.dynamic_slice_in_dim(all_slots, start, exp_count, axis=0)
    my_gates = lax.dynamic_slice_in_dim(all_gates, start, exp_count, axis=0)
    my_place = (my_slots[:, :, :, None] == columns).astype(jnp.float32)
    gates = jnp.sum(my_place * my_gates[:, :, :, None], axis=(1, 2))
    gates = gates.reshape(exp_count, local, capacity).transpose(1, 0, 2)
    gates = gates.reshape(local, exp_count * capacity, 1)

    sigmoid_gate = jax.nn.sigmoid(pre_gate)
    activated = pre_gate * sigmoid_gate
    hidden = activated * pre_up
    slot_gate = jnp.sum(hidden * projected, axis=2)
    delta_hidden = gates * projected
    delta_gate = delta_hidden * pre_up * sigmoid_gate * (1.0 + pre_gate * (1.0 - sigmoid_gate))
    delta_up = delta_hidden * activated
    deltas = jnp.concatenate([delta_gate, delta_up, gates * hidden], axis=2).astype(jnp.bfloat16)
    deltas = lax.all_gather(deltas, GROUP, axis=0, tiled=False)
    deltas = deltas.transpose(1, 0, 2, 3).reshape(local, sources * capacity, 3 * hidden_units)
    delta_in = deltas[:, :, : 2 * hidden_units]
    scaled_hidden = deltas[:, :, 2 * hidden_units :]

    slot_gate = slot_gate.reshape(local, exp_count, capacity).transpose(1, 0, 2)
    slot_gate = slot_gate.reshape(exp_count, 1, 1, local_slots)
    gate_part = jnp.sum(my_place * slot_gate, axis=3)
    gate_part = gate_part.astype(jnp.bfloat16).reshape(exp_count, token_count * 2)
    gate_part = lax.all_to_all(gate_part, "exp", split_axis=0, concat_axis=0, tiled=True)
    gate_grad = jnp.sum(gate_part.astype(jnp.float32), axis=0).astype(jnp.bfloat16)
    gate_grad = gate_grad.reshape(token_count, 2)

    slot_grads = jnp.einsum("esf,edf->esd", delta_in, w_in, preferred_element_type=jnp.float32)
    slot_grads = slot_grads.astype(jnp.bfloat16).reshape(local, sources, capacity, rows)
    slot_grads = slot_grads.transpose(1, 0, 2, 3).reshape(sources, local_slots, rows)
    returned = jnp.einsum("ntc,ncd->ntd", place, slot_grads, preferred_element_type=jnp.bfloat16)
    returned = returned.reshape(shares, exp_count, token_count, rows)
    returned = lax.all_to_all(returned, "exp", split_axis=1, concat_axis=1, tiled=True)
    returned = jnp.sum(returned.astype(jnp.float32), axis=1).astype(jnp.bfloat16)
    returned = lax.all_to_all(returned, GROUP, split_axis=0, concat_axis=0, tiled=True)
    token_grad = returned.transpose(1, 0, 2).reshape(token_count, width)

    grad_in = jnp.einsum("esd,esf->edf", inputs, delta_in, preferred_element_type=jnp.float32)
    grad_down = jnp.einsum(
        "esd,esf->edf", upstream, scaled_hidden, preferred_element_type=jnp.float32
    )
    gradient = jnp.stack([grad_in[:, :, :hidden_units], grad_in[:, :, hidden_units:], grad_down])
    new_params, new_first, new_second = adam_update(params, gradient, moment_first, moment_second)
    return (token_grad, gate_grad, new_params, new_first, new_second)


def solution(mesh):
    tokens_spec = P(("cuts", "exp", "fsdp"), None)
    weights_spec = P(None, "exp", ("cuts", "fsdp"), None)
    return jax.shard_map(
        per_device,
        mesh=mesh,
        in_specs=(tokens_spec,) * 4 + (weights_spec,) * 3,
        out_specs=(tokens_spec,) * 2 + (weights_spec,) * 3,
        check_vma=False,
    )
```

profile of v0, /device:TPU:0, one launch (start us, length us, event | category | flops | bytes accessed | tf_op | source)
XLA Modules:
  0.0 402.4 jit_solution(14626634083939528833)
XLA Ops:
  10.4 1.6 copy.214
  12.7 2.2 copy.219
  14.8 36.0 %all_to_all.46 = bf16[16,136,256]{2,1,0:T(8,128)(2,1)S(1)} all-to-all(bf16[16,136,256]{2,1,0:T(8,128)(2,1)} %copy.219), channel_id=1, replica_groups=mesh['cuts'=4,'exp'=2,'fsdp'=4] {'cuts','fsdp'}, dimensions={0} | all-to-all | bytes 2228224 | tf_op jit(solution)/shard_map/all_to_all | solution.py:57
  50.9 1.2 copy.220
  52.8 1.3 copy.231
  54.1 30.7 %all_to_all.47 = bf16[16,128,256]{2,1,0:T(8,128)(2,1)S(1)} all-to-all(bf16[16,128,256]{2,1,0:T(8,128)(2,1)} %copy.231), channel_id=1, replica_groups=mesh['cuts'=4,'exp'=2,'fsdp'=4] {'cuts','fsdp'}, dimensions={0} | all-to-all | bytes 2097152 | tf_op jit(solution)/shard_map/all_to_all | solution.py:57
  84.9 1.6 copy.232
  86.5 1.4 convert_element_type.97
  87.8 2.3 slice_bitcast_fusion.5
  90.1 2.4 copy.221
  92.5 1.6 slice.69
  94.1 6.8 %reshape.194 = bf16[32,3,128,2]{3,2,0,1:T(8,128)(2,1)S(1)} reshape(bf16[16,2,3,256]{3,1,0,2:T(2,128)(2,1)S(1)} %copy.222) | data formatting | bytes 98304 | tf_op jit(solution)/shard_map/reshape | solution.py:76
  100.9 1.9 fusion.38
  102.9 2.2 copy.223
  105.9 2.9 fusion.25
  109.0 0.8 copy-done.11
  110.2 1.5 convolution_convert_fusion
  112.3 9.1 %all_to_all.48 = bf16[2,2,4,4,80,512]{5,4,2,1,3,0:T(8,128)(2,1)} all-to-all(bf16[2,2,4,4,80,512]{5,4,2,1,3,0:T(8,128)(2,1)S(1)} %bitcast.88), channel_id=1, replica_groups={{0,8},{16,24},{1,9},{17,25},{2,10},{18,26},{3,11},{19,27},{4,12},{20,28..., dimensions={0} | all-to-all | bytes 10485760 | tf_op jit(solution)/shard_map/all_to_all | solution.py:96
  121.4 5.9 %reduce_sum.117 = bf16[2,4,4,80,512]{4,3,1,0,2:T(8,128)(2,1)} reduce(bf16[2,2,4,4,80,512]{5,4,2,1,3,0:T(8,128)(2,1)} %all_to_all.48, bf16[]{:T(256)} %constant.42.clone.1), dimensions={0}, to_apply=%region_5.6 | reduce | flops 1310720 | bytes 7864322 | tf_op jit(solution)/shard_map/reduce_sum | solution.py:99
  127.3 2.4 copy.233
  129.7 0.8 fusion.26
  130.7 2.3 convolution_convert_fusion.1
  133.2 6.8 %all_to_all.49 = bf16[2,2,4,4,80,256]{5,4,2,1,3,0:T(8,128)(2,1)} all-to-all(bf16[2,2,4,4,80,256]{5,4,2,1,3,0:T(8,128)(2,1)S(1)} %bitcast.97), channel_id=1, replica_groups={{0,8},{16,24},{1,9},{17,25},{2,10},{18,26},{3,11},{19,27},{4,12},{20,28..., dimensions={0} | all-to-all | bytes 5242880 | tf_op jit(solution)/shard_map/all_to_all | solution.py:96
  140.0 3.6 reduce_sum.118
  143.6 2.5 copy.237
  146.2 4.3 %all-to-all-start.4 = ((bf16[8,4,80,256]{3,2,1,0:T(8,128)(2,1)}), bf16[8,4,80,256]{3,2,1,0:T(8,128)(2,1)}, u32[]{:S(2)}, u32[]{:S(2)}) async-start(bf16[8,4,80,256]{3,2,1,0:T(8,128)(2,1)} %copy.237), calls=%async_computation.4 | async-start | bytes 2621440 | tf_op jit(solution)/shard_map/all_to_all | solution.py:103
  150.4 3.5 copy.238
  153.9 29.4 %all-to-all-done.4 = bf16[8,4,80,256]{3,2,1,0:T(8,128)(2,1)} async-done(((bf16[8,4,80,256]{3,2,1,0:T(8,128)(2,1)}), bf16[8,4,80,256]{3,2,1,0:T(8,128)(2,1)}, u32[]{:S(2)}, u32[]{:S(2)}) %all-to-all-start.4) | async-done | bytes 1310752 | tf_op jit(solution)/shard_map/all_to_all | solution.py:103
  183.3 4.4 %all-to-all-start.5 = ((bf16[8,4,80,512]{3,2,1,0:T(8,128)(2,1)}), bf16[8,4,80,512]{3,2,1,0:T(8,128)(2,1)}, u32[]{:S(2)}, u32[]{:S(2)}) async-start(bf16[8,4,80,512]{3,2,1,0:T(8,128)(2,1)} %copy.238), calls=%async_computation.5 | async-start | bytes 5242880 | tf_op jit(solution)/shard_map/all_to_all | solution.py:103
  188.7 1.5 convert_reduce_fusion.1
  190.2 57.6 %all-to-all-done.5 = bf16[8,4,80,512]{3,2,1,0:T(8,128)(2,1)} async-done(((bf16[8,4,80,512]{3,2,1,0:T(8,128)(2,1)}), bf16[8,4,80,512]{3,2,1,0:T(8,128)(2,1)}, u32[]{:S(2)}, u32[]{:S(2)}) %all-to-all-start.5) | async-done | bytes 2621472 | tf_op jit(solution)/shard_map/all_to_all | solution.py:103
  247.8 2.2 convert_reduce_fusion
  253.9 3.2 all-to-all-start.8
  257.1 63.2 %all-gather.6.cloned.1.call-done = bf16[16,4,80,768]{3,2,0,1:T(8,128)(2,1)} async-done(((bf16[1,4,80,768]{3,2,0,1:T(8,128)(2,1)}), bf16[16,4,80,768]{3,2,0,1:T(8,128)(2,1)}) %all-gather.6.cloned.1.call-update) | async-done | bytes 7864336 | tf_op jit(solution)/shard_map/all_gather | solution.py:132
  320.3 4.0 %fusion.5 = bf16[4,1280,256]{2,1,0:T(8,128)(2,1)S(1)} fusion(bf16[4,1280,768]{2,1,0:T(8,128)(2,1)} %bitcast.115, bf16[4,256,256]{2,1,0:T(8,128)(2,1)S(1)} %copy-done.14, bf16[4,256,256]{2,1,0:T(8,128)(2,1)S(1)} %copy-done.12), kind=kOutput, calls=%fused_computation.10 | convolution fusion | flops 1345585152 | bytes 8912896 | tf_op jit(solution)/shard_map/esf,edf->esd/dot_general | solution.py:145
  324.7 1.0 copy-done.2
  326.4 1.5 copy.242
  328.0 5.0 %all-to-all-start.6 = ((bf16[16,2,128,256]{3,2,0,1:T(8,128)(2,1)}), bf16[16,2,128,256]{3,2,0,1:T(8,128)(2,1)}, u32[]{:S(2)}, u32[]{:S(2)}) async-start(bf16[16,2,128,256]{3,2,0,1:T(8,128)(2,1)} %copy.242), calls=%async_computation.6 | async-start | bytes 4194304 | tf_op jit(solution)/shard_map/all_to_all | solution.py:150
  333.9 24.6 %all-to-all-done.6 = bf16[16,2,128,256]{3,2,0,1:T(8,128)(2,1)} async-done(((bf16[16,2,128,256]{3,2,0,1:T(8,128)(2,1)}), bf16[16,2,128,256]{3,2,0,1:T(8,128)(2,1)}, u32[]{:S(2)}, u32[]{:S(2)}) %all-to-all-start.6) | async-done | bytes 2097184 | tf_op jit(solution)/shard_map/all_to_all | solution.py:150
  358.4 3.3 reduce_sum.121
  361.7 4.3 %all-to-all-start.7 = ((bf16[16,128,256]{2,1,0:T(8,128)(2,1)}), bf16[16,128,256]{2,1,0:T(8,128)(2,1)}, u32[]{:S(2)}, u32[]{:S(2)}) async-start(bf16[16,128,256]{2,1,0:T(8,128)(2,1)} %reduce_sum.121), calls=%async_computation.7 | async-start | bytes 2097152 | tf_op jit(solution)/shard_map/all_to_all | solution.py:152
  366.0 4.2 %fusion.1 = f32[4,256,512]{2,1,0:T(8,128)S(1)} fusion(bf16[4,1280,256]{2,1,0:T(8,128)(2,1)S(1)} %bitcast.99, bf16[4,1280,768]{2,1,0:T(8,128)(2,1)} %bitcast.116), kind=kOutput, calls=%fused_computation.6 | convolution fusion | flops 1342177280 | bytes 9961472 | tf_op jit(solution)/shard_map/esd,esf->edf/dot_general | solution.py:155
  370.5 1.5 copy-done.6
  372.0 2.9 fusion.12
  375.6 4.8 %multiply_subtract_fusion = (f32[3,4,256,256]{3,2,1,0:T(8,128)}, f32[3,4,256,256]{3,2,1,0:T(8,128)}, f32[3,4,256,256]{3,2,1,0:T(8,128)}) fusion(f32[3,4,256,256]{3,2,1,0:T(8,128)S(1)} %copy-done.4, f32[1,4,256,256]{3,2,1,0:T(8,128)S(1)} %fusion.12, f32[1,4,256,256]{3,2,1,0:T(8,128)S(1)} %get-tuple-element.60, f32[1,4,256,256]{3,2,1,0:T(8,128)S(1)} %get-tuple-element.59, ...), kind=kLoop, calls=%fused_computation.14 | loop fusion | flops 13369344 | bytes 22020096 | tf_op jit(solution)/shard_map/sub | solution.py:23
  380.5 12.4 %all-to-all-done.7 = bf16[16,128,256]{2,1,0:T(8,128)(2,1)} async-done(((bf16[16,128,256]{2,1,0:T(8,128)(2,1)}), bf16[16,128,256]{2,1,0:T(8,128)(2,1)}, u32[]{:S(2)}, u32[]{:S(2)}) %all-to-all-start.7) | async-done | bytes 1048608 | tf_op jit(solution)/shard_map/all_to_all | solution.py:152
  392.9 1.6 copy.244
  394.5 1.3 copy.250
  (93 shorter events, 14.5 us)
Async XLA Ops:
  7.2 82.9 %all-gather.8.cloned.1.call-start = ((), (), s32[]{:S(2)}) async-start(), calls=%async_computation.10 | async-start | bytes 3342336 | tf_op jit(solution)/shard_map/all_gather | solution.py:58
  14.8 37.3 %copy-start.15 = (bf16[128,4096]{1,0:T(8,128)(2,1)S(1)}, bf16[128,4096]{1,0:T(8,128)(2,1)}, u32[]{:S(2)}) copy-start(bf16[128,4096]{1,0:T(8,128)(2,1)} %param.8) | copy-start | bytes 3145732
  52.1 75.1 %all-gather.10.cloned.1.call-start = ((), (), s32[]{:S(2)}) async-start(), calls=%async_computation.11 | async-start | bytes 3145728 | tf_op jit(solution)/shard_map/all_gather | solution.py:58
  54.1 32.3 %copy-start.3 = (f32[3,4,256,256]{3,2,1,0:T(8,128)S(1)}, f32[3,4,256,256]{3,2,1,0:T(8,128)}, u32[]{:S(2)}) copy-start(f32[3,4,256,256]{3,2,1,0:T(8,128)} %param.11) | copy-start | bytes 9437188
  105.8 2.9 copy-start
  108.8 1.0 copy-start.11
  108.8 1.4 copy-start.13
  109.0 2.8 copy-start.7
  127.3 2.4 copy-start.1
  130.7 2.3 copy-start.5
  146.2 37.1 %all-to-all-start.4 = ((bf16[8,4,80,256]{3,2,1,0:T(8,128)(2,1)}), bf16[8,4,80,256]{3,2,1,0:T(8,128)(2,1)}, u32[]{:S(2)}, u32[]{:S(2)}) async-start(bf16[8,4,80,256]{3,2,1,0:T(8,128)(2,1)} %copy.237), calls=%async_computation.4 | async-start | bytes 2621440 | tf_op jit(solution)/shard_map/all_to_all | solution.py:103
  183.3 64.5 %all-to-all-start.5 = ((bf16[8,4,80,512]{3,2,1,0:T(8,128)(2,1)}), bf16[8,4,80,512]{3,2,1,0:T(8,128)(2,1)}, u32[]{:S(2)}, u32[]{:S(2)}) async-start(bf16[8,4,80,512]{3,2,1,0:T(8,128)(2,1)} %copy.238), calls=%async_computation.5 | async-start | bytes 5242880 | tf_op jit(solution)/shard_map/all_to_all | solution.py:103
  187.7 132.6 %all-gather.6.cloned.1.call-start = ((), (), s32[]{:S(2)}) async-start(), calls=%async_computation.9 | async-start | bytes 8355840 | tf_op jit(solution)/shard_map/all_gather | solution.py:132
  249.9 70.4 %copy-start.12 = (bf16[4,256,256]{2,1,0:T(8,128)(2,1)S(1)}, bf16[4,256,256]{2,1,0:T(8,128)(2,1)}, u32[]{:S(2)}) copy-start(bf16[4,256,256]{2,1,0:T(8,128)(2,1)} %get-tuple-element.61) | copy-start | bytes 1572868
  249.9 70.4 %copy-start.14 = (bf16[4,256,256]{2,1,0:T(8,128)(2,1)S(1)}, bf16[4,256,256]{2,1,0:T(8,128)(2,1)}, u32[]{:S(2)}) copy-start(bf16[4,256,256]{2,1,0:T(8,128)(2,1)} %get-tuple-element.62) | copy-start | bytes 1572868
  253.9 74.1 %all-to-all-start.8 = ((bf16[2,2,128]{2,1,0:T(2,128)(2,1)}), bf16[2,2,128]{2,1,0:T(2,128)(2,1)S(1)}, u32[]{:S(2)}, u32[]{:S(2)}) async-start(bf16[2,2,128]{2,1,0:T(2,128)(2,1)} %reshape.217), calls=%async_computation.8 | async-start | bytes 2048 | tf_op jit(solution)/shard_map/all_to_all | solution.py:141
  324.4 1.3 copy-start.2
  328.0 30.4 %all-to-all-start.6 = ((bf16[16,2,128,256]{3,2,0,1:T(8,128)(2,1)}), bf16[16,2,128,256]{3,2,0,1:T(8,128)(2,1)}, u32[]{:S(2)}, u32[]{:S(2)}) async-start(bf16[16,2,128,256]{3,2,0,1:T(8,128)(2,1)} %copy.242), calls=%async_computation.6 | async-start | bytes 4194304 | tf_op jit(solution)/shard_map/all_to_all | solution.py:150
  333.8 32.2 %copy-start.8 = (bf16[32,4,40,256]{3,2,0,1:T(8,128)(2,1)S(1)}, bf16[32,4,40,256]{3,2,0,1:T(8,128)(2,1)}, u32[]{:S(2)}) copy-start(bf16[32,4,40,256]{3,2,0,1:T(8,128)(2,1)} %copy-done.7) | copy-start | bytes 7864324
  361.7 31.2 %all-to-all-start.7 = ((bf16[16,128,256]{2,1,0:T(8,128)(2,1)}), bf16[16,128,256]{2,1,0:T(8,128)(2,1)}, u32[]{:S(2)}, u32[]{:S(2)}) async-start(bf16[16,128,256]{2,1,0:T(8,128)(2,1)} %reduce_sum.121), calls=%async_computation.7 | async-start | bytes 2097152 | tf_op jit(solution)/shard_map/all_to_all | solution.py:152
  366.0 8.9 %copy-start.10 = (f32[3,4,256,256]{3,2,1,0:T(8,128)S(1)}, f32[3,4,256,256]{3,2,1,0:T(8,128)}, u32[]{:S(2)}) copy-start(f32[3,4,256,256]{3,2,1,0:T(8,128)} %param.13) | copy-start | bytes 9437188
  370.3 1.7 copy-start.6
  372.0 2.9 copy-start.4
  372.0 3.6 copy-start.9
Sparse Core Ops, SparseCore 0:
  52.2 33.0 all-gather.7
  87.4 33.0 all-gather.9
  251.9 68.3 all-gather.5
where the time goes:
time: 404 us; the launch traced here: 402 us
  waiting for transfers between devices  187 us (46%)
  blocking collectives  82.7 us (20%)
  local copies, waits for them, and re-layouts  48.1 us (12%)
  other arithmetic  29.4 us (7%)
  starting transfers between devices  21.4 us (5%)
  matrix products  19.4 us (5%)
  between operations  14.3 us (4%)
    all_to_all x2, waiting for transfers between devices, finish(): lax.all_to_all(out, GROUP, split_axis=0, concat_axis=0, tiled=True, axis_...  86.9 us
    all_to_all x2, blocking collectives, exchange(): lax.all_to_all(parts, GROUP, split_axis=0, concat_axis=0, tiled=True)  66.8 us
    all_gather x1, waiting for transfers between devices, per_device(): deltas = lax.all_gather(deltas, GROUP, axis=0, tiled=False)  63.2 us
    all_to_all x1, waiting for transfers between devices, per_device(): lax.all_to_all(returned, 'exp', split_axis=1, concat_axis=1, tiled=True)  24.6 us
    all_to_all x2, blocking collectives, partial_sums(): lax.all_to_all(out, 'cuts', split_axis=0, concat_axis=0, tiled=True, axis...  15.9 us
    all_to_all x1, waiting for transfers between devices, per_device(): lax.all_to_all(returned, GROUP, split_axis=0, concat_axis=0, tiled=True)  12.4 us
    unnamed x41, local copies, waits for them, and re-layouts  11 us
    reduce_sum x2, other arithmetic, partial_sums(): return jnp.sum(out.astype(jnp.float32), axis=0).astype(jnp.bfloat16)  9.5 us
  transfers between devices with their start and end apart: 8, of which 5 were waited for; matrix products, arithmetic and copies ran while one was open for 15% of the time, Pallas kernels for 0%

commit v1 on v0

v1 whole, which is shorter than its diff:
```python
import functools

import jax
import jax.numpy as jnp
from jax import lax
from jax.experimental import pallas as pl
from jax.experimental.pallas import tpu as pltpu
from jax.sharding import PartitionSpec as P

EXPERTS = 8
CORES = 2
MESH = pl.DeviceIdType.MESH

decay_first = 0.9
decay_second = 0.95
correct_first = 1.0 - 0.9**10
correct_second = 1.0 - 0.95**10
epsilon = 1e-08
learn_rate = 0.0003
weight_decay = 0.1


def adam_update(params, gradient, moment_first, moment_second):
    new_first = decay_first * moment_first + (1.0 - decay_first) * gradient
    new_second = decay_second * moment_second + (1.0 - decay_second) * gradient * gradient
    stepped = new_first / correct_first / (jnp.sqrt(new_second / correct_second) + epsilon)
    new_params = params - learn_rate * (stepped + weight_decay * params)
    return (new_params, new_first, new_second)


def loop(count, body):
    def step(i, carry):
        body(i)
        return carry

    lax.fori_loop(0, count, step, 0)


def dot(a, b, dims):
    return lax.dot_general(a, b, (dims, ((), ())), preferred_element_type=jnp.float32)


def kernel(
    sizes,
    info_ref, tok_ref, og_ref, w_ref,
    tg_ref, gg_ref, grad_ref,
    info, weights, tokb, ogb, place, inp, ups, pre_s, prj_s, pre_r, prj_r, own, dl, sg, ret_r, tg_s,
    gg_s, gg_r, g1_out, g1_in, g2_out, g2_in,
    si, ri, sz, rz, sy, ry, sw, rw, sv, rv, sp, rp, sa, ra, st, rt, so, ro, sg_sem, rg_sem, s1, r1, s2, r2,
    local_sem,
):
    nk, ne, nf, local, cap, tcount, rows, units = sizes
    chips = nk // CORES
    span = ne * cap
    slots = local * span
    depth = nk * rows
    bf = jnp.bfloat16
    f32 = jnp.float32
    k, e, f = lax.axis_index("cuts"), lax.axis_index("exp"), lax.axis_index("fsdp")
    x, c = k // CORES, lax.rem(k, CORES)

    def f_at(d):
        return lax.rem(f + d, nf)

    def e_at(d):
        return lax.rem(e + d, ne)

    def x_at(d):
        return lax.rem(x + d, chips)

    partner = x * CORES + 1 - c

    def put(src, dst, send, recv, device):
        return pltpu.make_async_remote_copy(
            src_ref=src, dst_ref=dst, send_sem=send, recv_sem=recv, device_id=device, device_id_type=MESH
        )

    def strip(kk, ff):
        return pl.ds(pl.multiple_of((kk * nf + ff) * rows, rows), rows)

    def cut(kk):
        return pl.ds(pl.multiple_of(kk * rows, rows), rows)

    def mine(ee):
        return pl.ds(pl.multiple_of(ee * tcount, tcount), tcount)

    def group(g):
        return pl.ds(pl.multiple_of(g * span, span), span)

    barrier = pltpu.get_barrier_semaphore()
    partners = 0
    for de in range(ne):
        for d in range(nf):
            if de or d:
                pl.semaphore_signal(barrier, inc=1, device_id=(k, e_at(de), f_at(d)), device_id_type=MESH)
                partners += 1
    pl.semaphore_signal(barrier, inc=1, device_id=(partner, e, f), device_id_type=MESH)
    partners += 1
    for dx in range(1, chips):
        pl.semaphore_signal(barrier, inc=1, device_id=(x_at(dx) * CORES + c, e, f), device_id_type=MESH)
        partners += 1
    pl.semaphore_wait(barrier, partners)

    def info_copy(de, d):
        return put(info_ref, info.at[f, e], si.at[de, d], ri.at[de, d], (k, e_at(de), f_at(d)))

    for de in range(ne):
        for d in range(nf):
            if de or d:
                info_copy(de, d).start()

    arrays = ((tok_ref, tokb), (og_ref, ogb))
    order = sorted(range(1, nf), key=lambda d: -min(d, nf - d))
    for a, (src, dst) in enumerate(arrays):
        for d in order:
            ff = f_at(d)
            for kk in range(nk):
                put(
                    src.at[:, strip(kk, ff)], dst.at[f, mine(e), cut(kk)], sz.at[a, d], rz.at[a, d], (k, e, ff)
                ).start()
        for de in range(1, ne):
            for kk in range(nk):
                put(
                    src.at[:, strip(kk, f)], dst.at[f, mine(e), cut(kk)], sy.at[a, f, de], ry.at[a, f, de],
                    (k, e_at(de), f),
                ).start()
        if a == 0:
            for dx in range(1, chips):
                put(
                    w_ref, weights.at[:, cut(k), :], sw.at[dx], rw.at[dx], (x_at(dx) * CORES + c, e, f)
                ).start()
            put(w_ref, weights.at[:, cut(k), :], sv.at[0], rv.at[0], (partner, e, f)).start()

    info[f, e] = info_ref[...]
    for src, dst in arrays:
        for kk in range(nk):
            dst[f, mine(e), cut(kk)] = src[:, strip(kk, f)]
    weights[:, cut(k), :] = w_ref[...]

    def whole(a, dst, g, ee, send, recv, device):
        return put(dst.at[g, mine(ee), :], dst.at[g, mine(ee), :], send, recv, device)

    for a, (src, dst) in enumerate(arrays):
        for d in order:
            g = f_at(nf - d)
            whole(a, dst, g, e, sz.at[a, d], rz.at[a, d], (k, e, f_at(d))).wait_recv()
            for de in range(1, ne):
                whole(a, dst, g, e, sy.at[a, g, de], ry.at[a, g, de], (k, e_at(de), f)).start()
        if a == 0:
            for de in range(ne):
                for d in range(nf):
                    if de or d:
                        info_copy(de, d).wait_recv()

    for dx in range(1, chips):
        held = weights.at[:, cut(x_at(chips - dx) * CORES + c), :]
        put(w_ref, held, sw.at[dx], rw.at[dx], (x_at(dx) * CORES + c, e, f)).wait_recv()
        put(held, held, sv.at[dx], rv.at[dx], (partner, e, f)).start()
    for dx in range(chips):
        held = weights.at[:, cut(x_at(chips - dx) * CORES + 1 - c), :]
        put(held, held, sv.at[dx], rv.at[dx], (partner, e, f)).wait_recv()

    def codes(g, row):
        return jnp.concatenate([info[g, ee, row : row + 1, :] for ee in range(ne)], axis=1)

    first_slot = (e * slots).astype(f32)

    def choose(g, base, count):
        ids = lax.broadcasted_iota(jnp.int32, (count, ne * tcount), 0).astype(f32) + base
        return [codes(g, j) - first_slot == ids for j in range(2)]

    def picked(a, src, dst, g):
        for de in range(1, ne):
            ee = e_at(ne - de)
            whole(a, src, g, ee, sy.at[a, g, de], ry.at[a, g, de], (k, e_at(de), f)).wait_recv()

        def column(kk):
            out = dot(place[g], src[g, :, cut(kk)], ((1,), (0,))).astype(bf)
            for l in range(local):
                dst[l, group(g), cut(kk)] = out[l * span : (l + 1) * span]

        loop(nk, column)

    def rs_copy(a, d):
        sent, got = ((pre_s, pre_r), (prj_s, prj_r))[a]
        g = f_at(d)
        return put(sent.at[g], got.at[d], sp.at[a, d], rp.at[a, d], (k, e, g))

    def forward(i):
        d = lax.rem(i + 1, nf)
        g = f_at(d)
        zero, one = choose(g, 0.0, slots)
        place[g] = jnp.where(zero, 1.0, 0.0).astype(bf) + jnp.where(one, 1.0, 0.0).astype(bf)
        picked(0, tokb, inp, g)

        def expert(l):
            out = dot(inp[l, group(g), :], weights[l, :, : 2 * units], ((1,), (0,)))
            own[pl.ds(pl.multiple_of(l * span, span), span), : 2 * units] = out
            pre_s[g, pl.ds(pl.multiple_of(l * span, span), span), :] = out.astype(bf)

        loop(local, expert)

        @pl.when(d > 0)
        def _():
            rs_copy(0, d).start()

    loop(nf, forward)

    def backward(i):
        d = lax.rem(i + 1, nf)
        g = f_at(d)
        picked(1, ogb, ups, g)

        def expert(l):
            out = dot(ups[l, group(g), :], weights[l, :, 2 * units :], ((1,), (0,)))
            own[pl.ds(pl.multiple_of(l * span, span), span), 2 * units :] = out
            prj_s[g, pl.ds(pl.multiple_of(l * span, span), span), :] = out.astype(bf)

        loop(local, expert)

        @pl.when(d > 0)
        def _():
            rs_copy(1, d).start()

    loop(nf, backward)

    for a in range(2):
        for d in range(1, nf):
            rs_copy(a, d).wait_recv()

    def middle(l, carry):
        here = pl.ds(pl.multiple_of(l * span, span), span)
        gate = own[here, :units]
        up = own[here, units : 2 * units]
        proj = own[here, 2 * units :]
        for d in range(1, nf):
            gate += pre_r[d, here, :units].astype(f32)
            up += pre_r[d, here, units:].astype(f32)
            proj += prj_r[d, here, :].astype(f32)
        zero, one = choose(f, (l * span).astype(f32), span)
        scale = jnp.sum(
            jnp.where(zero, codes(f, 2), 0.0) + jnp.where(one, codes(f, 3), 0.0), axis=1, keepdims=True
        )
        sig = jax.nn.sigmoid(gate)
        act = gate * sig
        hidden = act * up
        slot_gate = jnp.sum(hidden * proj, axis=1, keepdims=True)
        delta = scale * proj
        dl[l, group(f), :units] = (delta * up * sig * (1.0 + gate * (1.0 - sig))).astype(bf)
        dl[l, group(f), units : 2 * units] = (delta * act).astype(bf)
        dl[l, group(f), 2 * units :] = (scale * hidden).astype(bf)
        return (
            carry[0] + jnp.sum(jnp.where(zero, slot_gate, 0.0), axis=0, keepdims=True),
            carry[1] + jnp.sum(jnp.where(one, slot_gate, 0.0), axis=0, keepdims=True),
        )

    nothing = jnp.zeros((1, ne * tcount), f32)
    parts = lax.fori_loop(0, local, middle, (nothing, nothing))

    def ag_copy(d):
        held = dl.at[:, group(f), :]
        return put(held, held, sa.at[d], ra.at[d], (k, e, f_at(d)))

    for d in order:
        ag_copy(d).start()

    for ee in range(ne):
        for j in range(2):
            gg_s[ee, j : j + 1, :] = parts[j][:, ee * tcount : (ee + 1) * tcount]

    def gg_copy(de):
        return put(gg_s.at[e_at(de)], gg_r.at[de], sg_sem.at[de], rg_sem.at[de], (k, e_at(de), f))

    for de in range(1, ne):
        gg_copy(de).start()

    for de in range(1, ne):
        for g in range(nf):
            whole(0, tokb, g, e, sy.at[0, g, de], ry.at[0, g, de], (k, e_at(de), f)).wait_send()

    def ret_copy(g, de):
        ee = e_at(de)
        return put(tokb.at[g, mine(ee), :], ret_r.at[g, de], st.at[g, de], rt.at[g, de], (k, ee, f))

    def returned(d):
        g = f_at(nf - d)

        @pl.when(d > 0)
        def _():
            held = dl.at[:, group(g), :]
            put(held, held, sa.at[d], ra.at[d], (k, e, f_at(d))).wait_recv()

        def column(kk):
            for l in range(local):
                sg[l * span : (l + 1) * span, :] = dot(
                    dl[l, group(g), : 2 * units], weights[l, cut(kk), : 2 * units], ((1,), (1,))
                ).astype(bf)
            tokb[g, :, cut(kk)] = dot(place[g], sg[...], ((0,), (0,))).astype(bf)

        loop(nk, column)
        for de in range(1, ne):
            ret_copy(g, de).start()

    loop(nf, returned)

    def gradient(kk, l):
        ahead = dot(inp[l, :, cut(kk)], dl[l, :, : 2 * units], ((0,), (0,)))
        down = dot(ups[l, :, cut(kk)], dl[l, :, 2 * units :], ((0,), (0,)))
        return ahead, down

    def g1_copy(dx, l):
        return put(g1_out.at[dx, l], g1_in.at[dx, l], s1.at[dx, l], r1.at[dx, l], (partner, e, f))

    def g2_copy(dx, l):
        return put(
            g2_out.at[dx, l], g2_in.at[dx, l], s2.at[dx, l], r2.at[dx, l], (x_at(dx) * CORES + c, e, f)
        )

    for dx in [*range(1, chips), 0]:

        def share(l):
            ahead, down = gradient(x_at(dx) * CORES + 1 - c, l)
            g1_out[dx, l, :, : 2 * units] = ahead.astype(bf)
            g1_out[dx, l, :, 2 * units :] = down.astype(bf)
            g1_copy(dx, l).start()
            ahead, down = gradient(x_at(dx) * CORES + c, l)
            g1_copy(dx, l).wait_recv()
            ahead += g1_in[dx, l, :, : 2 * units].astype(f32)
            down += g1_in[dx, l, :, 2 * units :].astype(f32)
            if dx:
                g2_out[dx, l, :, : 2 * units] = ahead.astype(bf)
                g2_out[dx, l, :, 2 * units :] = down.astype(bf)
                g2_copy(dx, l).start()
            else:
                grad_ref[0, l] = ahead[:, :units]
                grad_ref[1, l] = ahead[:, units:]
                grad_ref[2, l] = down

        loop(local, share)

    def tg_wait(d):
        return put(tg_s.at[0], tg_s.at[0], so.at[d], ro.at[d], (k, e, f_at(d)))

    def final(d):
        g = f_at(nf - d)
        total = tokb[g, mine(e), :].astype(f32)
        for de in range(1, ne):
            put(ret_r.at[g, de], ret_r.at[g, de], st.at[g, de], rt.at[g, de], (k, e_at(de), f)).wait_recv()
            total += ret_r[g, de].astype(f32)
        tg_s[g] = total.astype(bf)
        for kk in range(nk):
            there = tg_ref.at[:, strip(kk, f)]

            @pl.when(d > 0)
            def _():
                put(
                    tg_s.at[g, :, cut(kk)], there, so.at[nf - d], ro.at[nf - d], (k, e, g)
                ).start()

            @pl.when(d == 0)
            def _():
                pltpu.make_async_copy(tg_s.at[g, :, cut(kk)], there, local_sem).start()

    loop(nf, final)

    total = [gg_s[e, j : j + 1, :] for j in range(2)]
    for de in range(1, ne):
        gg_copy(de).wait_recv()
        for j in range(2):
            total[j] += gg_r[de, j : j + 1, :]
    for j in range(2):
        gg_ref[j : j + 1, :] = total[j]

    def collect(l):
        for dx in range(1, chips):
            g2_copy(dx, l).wait_recv()
            got = g2_in[dx, l].astype(f32)
            for part in range(3):
                grad_ref[part, l] += got[:, part * units : (part + 1) * units]

    loop(local, collect)

    for d in range(1, nf):
        tg_wait(d).wait()
    pltpu.make_async_copy(tg_s.at[0], tg_s.at[0], local_sem).wait()

    for de in range(ne):
        for d in range(nf):
            if de or d:
                info_copy(de, d).wait_send()
    for d in range(1, nf):
        for a, (src, dst) in enumerate(arrays):
            whole(a, dst, f, e, sz.at[a, d], rz.at[a, d], (k, e, f_at(d))).wait_send()
            rs_copy(a, d).wait_send()
        ag_copy(d).wait_send()
    for de in range(1, ne):
        gg_copy(de).wait_send()
        for g in range(nf):
            whole(1, ogb, g, e, sy.at[1, g, de], ry.at[1, g, de], (k, e_at(de), f)).wait_send()
            ret_copy(g, de).wait_send()
    for dx in range(chips):
        put(w_ref, w_ref, sv.at[dx], rv.at[dx], (partner, e, f)).wait_send()
        if dx:
            put(w_ref, w_ref, sw.at[dx], rw.at[dx], (partner, e, f)).wait_send()

        def sent(l):
            g1_copy(dx, l).wait_send()
            if dx:
                g2_copy(dx, l).wait_send()

        loop(local, sent)


def per_device(mesh_shape, tokens, out_grad, expert_ids, gate_probs, params, moment_first, moment_second):
    nk, ne, nf = mesh_shape["cuts"], mesh_shape["exp"], mesh_shape["fsdp"]
    token_count, width = tokens.shape
    local, rows, units = params.shape[1:]
    cap = 10 * token_count // 32
    chips = nk // CORES
    span = ne * cap
    slots = local * span
    depth = nk * rows
    bf, f32 = jnp.bfloat16, jnp.float32

    weights = params.astype(bf)
    w_block = jnp.concatenate([weights[0], weights[1], weights[2]], axis=2)

    flat_ids = expert_ids.reshape(-1)
    onehot = (flat_ids[:, None] == jnp.arange(EXPERTS, dtype=jnp.int32)).astype(jnp.int32)
    before = jnp.cumsum(onehot, axis=0) - onehot
    position = jnp.sum(before * onehot, axis=1)
    code = flat_ids * span + lax.axis_index("exp") * cap + position
    info = jnp.concatenate(
        [
            code.reshape(token_count, 2).T.astype(f32),
            gate_probs.T.astype(f32),
            jnp.zeros((4, token_count), f32),
        ]
    )

    sizes = (nk, ne, nf, local, cap, token_count, rows, units)
    vm = lambda shape, kind=bf: pltpu.VMEM(shape, kind)
    sem = lambda *shape: pltpu.SemaphoreType.DMA(shape)
    scratch = [
        vm((nf, ne, 8, token_count), f32),
        vm((local, depth, 3 * units)),
        vm((nf, ne * token_count, depth)),
        vm((nf, ne * token_count, depth)),
        vm((nf, slots, ne * token_count)),
        vm((local, nf * span, depth)),
        vm((local, nf * span, depth)),
        vm((nf, slots, 2 * units)),
        vm((nf, slots, units)),
        vm((nf, slots, 2 * units)),
        vm((nf, slots, units)),
        vm((slots, 3 * units), f32),
        vm((local, nf * span, 3 * units)),
        vm((slots, rows)),
        vm((nf, ne, token_count, depth)),
        vm((nf, token_count, depth)),
        vm((ne, 8, token_count), f32),
        vm((ne, 8, token_count), f32),
        vm((chips, local, rows, 3 * units)),
        vm((chips, local, rows, 3 * units)),
        vm((chips, local, rows, 3 * units)),
        vm((chips, local, rows, 3 * units)),
        sem(ne, nf), sem(ne, nf),
        sem(2, nf), sem(2, nf),
        sem(2, nf, ne), sem(2, nf, ne),
        sem(chips), sem(chips),
        sem(chips), sem(chips),
        sem(2, nf), sem(2, nf),
        sem(nf), sem(nf),
        sem(nf, ne), sem(nf, ne),
        sem(nf), sem(nf),
        sem(ne), sem(ne),
        sem(chips, local), sem(chips, local),
        sem(chips, local), sem(chips, local),
        pltpu.SemaphoreType.DMA,
    ]
    vmem = pl.BlockSpec(memory_space=pltpu.VMEM)
    token_grad, gates, gradient = pl.pallas_call(
        functools.partial(kernel, sizes),
        out_shape=(
            jax.ShapeDtypeStruct((token_count, width), bf),
            jax.ShapeDtypeStruct((8, token_count), f32),
            jax.ShapeDtypeStruct((3, local, rows, units), f32),
        ),
        in_specs=[vmem] * 4,
        out_specs=(pl.BlockSpec(memory_space=pl.ANY), vmem, vmem),
        scratch_shapes=scratch,
        compiler_params=pltpu.CompilerParams(
            collective_id=0, has_side_effects=True, vmem_limit_bytes=67043328
        ),
    )(info, tokens, out_grad, w_block)
    gate_grad = gates[:2].T.astype(bf)
    new_params, new_first, new_second = adam_update(params, gradient, moment_first, moment_second)
    return (token_grad, gate_grad, new_params, new_first, new_second)


def solution(mesh):
    tokens_spec = P(("cuts", "exp", "fsdp"), None)
    weights_spec = P(None, "exp", ("cuts", "fsdp"), None)
    return jax.shard_map(
        functools.partial(per_device, dict(mesh.shape)),
        mesh=mesh,
        in_specs=(tokens_spec,) * 4 + (weights_spec,) * 3,
        out_specs=(tokens_spec,) * 2 + (weights_spec,) * 3,
        check_vma=False,
    )
```

time: 404 us -> 221 us (0.55)
  Pallas kernels: 0 us -> 202 us
  waiting for transfers between devices: 187 us -> 0 us
  blocking collectives: 82.7 us -> 0 us
  local copies, waits for them, and re-layouts: 48.1 us -> 3.15 us
  starting transfers between devices: 21.4 us -> 0 us
  matrix products: 19.4 us -> 0 us
  other arithmetic: 29.4 us -> 14.7 us
  between operations: 14.3 us -> 0.7 us
    pallas_call x0 -> x1, Pallas kernels: none -> 202 us  [per_device(): pl.pallas_call(functools.partial(kernel, sizes), out_shape=(jax.ShapeDtyp...]
    all_to_all x5 -> x0, waiting for transfers between devices: 124 us -> none  [the longest x2 86.9 us: finish(): lax.all_to_all(out, GROUP, split_axis=0, concat_axis=0, tiled=True, axis_...]
    all_to_all x4 -> x0, blocking collectives: 82.7 us -> none  [the longest x2 66.8 us: exchange(): lax.all_to_all(parts, GROUP, split_axis=0, concat_axis=0, tiled=True)]
    all_gather x3 -> x0, waiting for transfers between devices: 63.2 us -> none  [the longest x1 63.2 us: per_device(): deltas = lax.all_gather(deltas, GROUP, axis=0, tiled=False)]
    all_to_all x5 -> x0, starting transfers between devices: 21.3 us -> none  [the longest x2 8.68 us: finish(): lax.all_to_all(out, GROUP, split_axis=0, concat_axis=0, tiled=True, axis_...]
    dot_general x8 -> x0, matrix products: 19.4 us -> none  [the longest x1 4.2 us: per_device(): jnp.einsum('esd,esf->edf', inputs, delta_in, preferred_element_type=jnp.f...]
    reduce_sum x9 -> x0, other arithmetic: 17.7 us -> none  [the longest x2 9.5 us: partial_sums(): return jnp.sum(out.astype(jnp.float32), axis=0).astype(jnp.bfloat16)]
    reshape x14 -> x0, local copies, waits for them, and re-layouts: 16 us -> none  [the longest x1 6.79 us: per_device(): everyone = everyone.reshape(sources, 3, token_count, 2)]
  transfers between devices with their start and end apart: 8 -> 0, of which waited for: 5 -> 0; matrix products, arithmetic and copies ran while one was open for 15% -> 0% of each run, Pallas kernels for 0% -> 0%
where the time goes in v1:
time: 221 us
  Pallas kernels  202 us (91%)
  other arithmetic  14.7 us (7%)
  local copies, waits for them, and re-layouts  3.15 us (1%)
    pallas_call x1, Pallas kernels, per_device(): pl.pallas_call(functools.partial(kernel, sizes), out_shape=(jax.ShapeDtyp...  202 us
    sub x1, other arithmetic, adam_update(): new_params = params - learn_rate * (stepped + weight_decay * params)  8 us

profile of v1, /device:TPU:0, one launch (start us, length us, event | category | flops | bytes accessed | tf_op | source)
XLA Modules:
  0.0 221.0 jit_solution(12687931615081312954)
XLA Ops:
  0.6 0.1 pad.5.clone
  0.7 0.7 convert_bitcast_fusion
  1.4 0.8 copy.12
  2.2 0.1 eq.29
  2.3 0.1 eq.25
  2.5 0.6 reduce-window.6
  3.0 0.2 slice_reduce_fusion
  3.3 0.1 fusion.2
  3.4 0.1 reduce_sum.12
  3.5 0.1 copy.14
  3.6 0.7 convert_bitcast_fusion.1
  4.3 0.7 maximum_maximum_fusion.info_ref
  5.0 2.1 convert_element_type.32
  7.0 0.1 slice_bitcast_fusion.2
  7.2 1.2 pad_maximum_fusion.w_ref
  8.4 202.4 %shard_map.110 = (bf16[128,4096]{1,0:T(8,128)(2,1)}, f32[8,128]{1,0:T(8,128)}, f32[3,4,256,256]{3,2,1,0:T(8,128)}) custom-call(f32[8,128]{1,0:T(8,128)} %maximum_maximum_fusion.info_ref, bf16[128,4096]{1,0:T(8,128)(2,1)} %tok_ref.1, bf16[128,4096]{1,0:T(8,128)(2,1)} %og_ref.1, bf16[4,256,768]{2,1,0:T(8,128)(2,1)} %pad_maximum_fusion.w_ref), custom_call_target="tpu_custom_call" | custom-call | tf_op jit(solution)/shard_map/pallas_call | solution.py:482
  210.8 0.7 convert.4
  211.5 0.5 slice_bitcast_fusion.3
  212.0 0.0 copy-start
  212.0 8.0 %multiply_subtract_fusion = (f32[3,4,256,256]{3,2,1,0:T(8,128)}, f32[3,4,256,256]{3,2,1,0:T(8,128)}, f32[3,4,256,256]{3,2,1,0:T(8,128)}) fusion(f32[3,4,256,256]{3,2,1,0:T(8,128)} %param.11, f32[3,4,256,256]{3,2,1,0:T(8,128)} %get-tuple-element.10, f32[3,4,256,256]{3,2,1,0:T(8,128)} %param.12, f32[3,4,256,256]{3,2,1,0:T(8,128)} %param.13), kind=kLoop, calls=%fused_computation.2 | loop fusion | flops 11796480 | bytes 22020096 | tf_op jit(solution)/shard_map/sub | solution.py:27
  220.0 0.0 copy-done
  220.0 1.0 copy.16
  (4 shorter events, 0.1 us)
Async XLA Ops:
  212.0 8.0 %copy-start = (bf16[128,4096]{1,0:T(8,128)(2,1)S(1)}, bf16[128,4096]{1,0:T(8,128)(2,1)}, u32[]{:S(2)}) copy-start(bf16[128,4096]{1,0:T(8,128)(2,1)} %get-tuple-element.22) | copy-start | bytes 3145732

commit v2 on v1

v2 whole, which is shorter than its diff:
```python
import functools

import jax
import jax.numpy as jnp
from jax import lax
from jax.experimental import pallas as pl
from jax.experimental.pallas import tpu as pltpu
from jax.sharding import PartitionSpec as P

CORES = 2
MESH = pl.DeviceIdType.MESH

decay_first = 0.9
decay_second = 0.95
correct_first = 1.0 - 0.9**10
correct_second = 1.0 - 0.95**10
epsilon = 1e-08
learn_rate = 0.0003
weight_decay = 0.1


def adam_update(params, gradient, moment_first, moment_second):
    new_first = decay_first * moment_first + (1.0 - decay_first) * gradient
    new_second = decay_second * moment_second + (1.0 - decay_second) * gradient * gradient
    stepped = new_first / correct_first / (jnp.sqrt(new_second / correct_second) + epsilon)
    new_params = params - learn_rate * (stepped + weight_decay * params)
    return (new_params, new_first, new_second)


def loop(count, body):
    def step(i, carry):
        body(i)
        return carry

    lax.fori_loop(0, count, step, 0)


def dot(a, b, dims):
    return lax.dot_general(a, b, (dims, ((), ())), preferred_element_type=jnp.float32)


def kernel(
    sizes,
    ids_ref, gates_ref, tok_hbm, og_hbm, params_hbm,
    tg_ref, gg_ref, grad_ref,
    tok_ref, og_ref, par_ref, info, weights, tokb, ogb, place, inp, ups, pre_s, prj_s, pre_r, prj_r, own, dl, sg,
    ret_r, tg_s, gg_s, gg_r, g1_out, g1_in, g2_out, g2_in,
    si, ri, sz, rz, sy, ry, sw, rw, sv, rv, sp, rp, sa, ra, st, rt, so, ro, sg_sem, rg_sem, s1, r1, s2, r2,
    own_sems,
):
    nk, ne, nf, local, cap, tcount, rows, units = sizes
    chips = nk // CORES
    span = ne * cap
    slots = local * span
    halves = 2 if local % 2 == 0 else 1
    part = local // halves
    bf = jnp.bfloat16
    f32 = jnp.float32
    k, e, f = lax.axis_index("cuts"), lax.axis_index("exp"), lax.axis_index("fsdp")
    x, c = k // CORES, lax.rem(k, CORES)
    scope = jax.named_scope

    def f_at(d):
        return lax.rem(f + d, nf)

    def e_at(d):
        return lax.rem(e + d, ne)

    def chip_at(d, core):
        return lax.rem(x + d, chips) * CORES + core

    partner = x * CORES + 1 - c

    def put(src, dst, send, recv, device):
        return pltpu.make_async_remote_copy(
            src_ref=src, dst_ref=dst, send_sem=send, recv_sem=recv, device_id=device, device_id_type=MESH
        )

    def strip(kk, ff):
        return pl.ds(pl.multiple_of((kk * nf + ff) * rows, rows), rows)

    def cut(kk):
        return pl.ds(pl.multiple_of(kk * rows, rows), rows)

    def mine(ee):
        return pl.ds(pl.multiple_of(ee * tcount, tcount), tcount)

    def group(g):
        return pl.ds(pl.multiple_of(g * span, span), span)

    barrier = pltpu.get_barrier_semaphore()
    partners = 0
    for de in range(ne):
        for d in range(nf):
            if de or d:
                pl.semaphore_signal(barrier, inc=1, device_id=(k, e_at(de), f_at(d)), device_id_type=MESH)
                partners += 1
    pl.semaphore_signal(barrier, inc=1, device_id=(partner, e, f), device_id_type=MESH)
    partners += 1
    for dx in range(1, chips):
        pl.semaphore_signal(barrier, inc=1, device_id=(chip_at(dx, c), e, f), device_id_type=MESH)
        partners += 1

    staged = ((tok_hbm, tok_ref), (og_hbm, og_ref), (params_hbm, par_ref))
    for n, (src, dst) in enumerate(staged):
        pltpu.make_async_copy(src, dst, own_sems.at[n]).start()

    def iota(shape, dim):
        return lax.broadcasted_iota(jnp.int32, shape, dim)

    experts = iota((local * ne, tcount), 0)
    named = [jnp.where(experts == ids_ref[j : j + 1, :], 1.0, 0.0).astype(f32) for j in range(2)]
    earlier = jnp.where(iota((tcount, tcount), 0) < iota((tcount, tcount), 1), 1.0, 0.0).astype(bf)
    before = dot((named[0] + named[1]).astype(bf), earlier, ((1,), (0,)))
    info[f, e] = jnp.zeros((8, tcount), f32)
    for j in range(2):
        position = jnp.sum(named[j] * before, axis=0, keepdims=True)
        info[f, e, j : j + 1, :] = (ids_ref[j : j + 1, :] * span + e * cap).astype(f32) + position
        info[f, e, j + 2 : j + 3, :] = gates_ref[j : j + 1, :].astype(f32)

    pltpu.make_async_copy(params_hbm, par_ref, own_sems.at[2]).wait()
    for l in range(local):
        for n in range(3):
            weights[l, cut(k), n * units : (n + 1) * units] = par_ref[n, l].astype(bf)
    for n, (src, dst) in enumerate(staged[:2]):
        pltpu.make_async_copy(src, dst, own_sems.at[n]).wait()
    with scope("barrier"):
        pl.semaphore_wait(barrier, partners)

    def info_copy(de, d):
        mark = info.at[f, e]
        return put(mark, mark, si.at[de, d], ri.at[de, d], (k, e_at(de), f_at(d)))

    order = sorted(range(1, nf), key=lambda d: -min(d, nf - d))
    arrays = ((tok_ref, tokb), (og_ref, ogb))
    wide = (pl.ds(0, 2 * units), pl.ds(2 * units, units))

    def z_start(a, d):
        src, dst = arrays[a]
        for kk in range(nk):
            put(
                src.at[:, strip(kk, f_at(d))], dst.at[f, mine(e), cut(kk)], sz.at[a, d], rz.at[a, d],
                (k, e, f_at(d)),
            ).start()

    def y_own_start(a):
        src, dst = arrays[a]
        for de in range(1, ne):
            for kk in range(nk):
                put(
                    src.at[:, strip(kk, f)], dst.at[f, mine(e), cut(kk)], sy.at[a, f, de], ry.at[a, f, de],
                    (k, e_at(de), f),
                ).start()

    def w_chip(a, dx, owner):
        held = weights.at[:, cut(owner), wide[a]]
        return put(held, held, sw.at[a, dx], rw.at[a, dx], (chip_at(dx, c), e, f))

    def w_core(a, dx, owner):
        held = weights.at[:, cut(owner), wide[a]]
        return put(held, held, sv.at[a, dx], rv.at[a, dx], (partner, e, f))

    def whole(dst, g, ee, send, recv, device):
        return put(dst.at[g, mine(ee), :], dst.at[g, mine(ee), :], send, recv, device)

    def z_whole(a, d):
        return whole(arrays[a][1], f_at(nf - d), e, sz.at[a, d], rz.at[a, d], (k, e, f_at(d)))

    def y_whole(a, g, de, ee):
        return whole(arrays[a][1], g, ee, sy.at[a, g, de], ry.at[a, g, de], (k, e_at(de), f))

    def z_pass(a, d):
        with scope("wait_z"):
            z_whole(a, d).wait_recv()
        for de in range(1, ne):
            y_whole(a, f_at(nf - d), de, e).start()

    for de in range(ne):
        for d in range(nf):
            if de or d:
                info_copy(de, d).start()
    for d in order:
        z_start(0, d)
    y_own_start(0)
    for a in range(2):
        for dx in range(1, chips):
            w_chip(a, dx, k).start()
        w_core(a, 0, k).start()
        if a == 0:
            for d in order:
                z_start(1, d)

    for src, dst in arrays:
        for kk in range(nk):
            dst[f, mine(e), cut(kk)] = src[:, strip(kk, f)]

    for n, d in enumerate(order):
        z_pass(0, d)
        if n == 0:
            y_own_start(1)
    for de in range(ne):
        for d in range(nf):
            if de or d:
                info_copy(de, d).wait_recv()

    def w_pass(a):
        with scope("wait_w"):
            for dx in range(1, chips):
                owner = chip_at(chips - dx, c)
                w_chip(a, dx, owner).wait_recv()
                w_core(a, dx, owner).start()
            for dx in range(chips):
                w_core(a, dx, chip_at(chips - dx, 1 - c)).wait_recv()

    def codes(g, row):
        return jnp.concatenate([info[g, ee, row : row + 1, :] for ee in range(ne)], axis=1)

    first_slot = (e * slots).astype(f32)

    def choose(g, base, count):
        ids = iota((count, ne * tcount), 0).astype(f32) + base
        return [codes(g, j) - first_slot == ids for j in range(2)]

    def at(l):
        return pl.ds(pl.multiple_of(l * span, span), span)

    def picked(a, dst, g):
        src = arrays[a][1]
        for de in range(1, ne):
            with scope("wait_y"):
                y_whole(a, g, de, e_at(ne - de)).wait_recv()

        def column(kk):
            out = dot(place[g], src[g, :, cut(kk)], ((1,), (0,))).astype(bf)
            for l in range(local):
                dst[l, group(g), cut(kk)] = out[l * span : (l + 1) * span]

        loop(nk, column)

    def partial_sum(a, g):
        with scope("partial"):
            if a == 0:
                zero, one = choose(g, 0.0, slots)
                place[g] = jnp.where(zero, 1.0, 0.0).astype(bf) + jnp.where(one, 1.0, 0.0).astype(bf)
            rows_of, sums = ((inp, pre_s), (ups, prj_s))[a]
            picked(a, rows_of, g)

            def expert(l):
                out = dot(rows_of[l, group(g), :], weights[l, :, wide[a]], ((1,), (0,)))
                own[at(l), wide[a]] = out
                sums[g, at(l), :] = out.astype(bf)

            loop(local, expert)

    def rs_copy(a, g, sign):
        sent, got = ((pre_s, pre_r), (prj_s, prj_r))[a]
        spot = jnp.where((sign < 0) & (g == f - 1), nf, g)
        return put(sent.at[g], got.at[spot], sp.at[a, g], rp.at[a, spot], (k, e, f + sign))

    def rs_wait(a, spot):
        got = (pre_r, prj_r)[a]
        put(got.at[spot], got.at[spot], sp.at[a, 0], rp.at[a, spot], (k, e, f_at(1))).wait_recv()

    def rs_step(a, g, sign):
        sent, got = ((pre_s, pre_r), (prj_s, prj_r))[a]
        behind = f - sign

        @pl.when((g - f) * sign > 0)
        def _():
            @pl.when((behind >= 0) & (behind < nf))
            def _():
                with scope("wait_rs"):
                    rs_wait(a, g)

                def add(l):
                    sent[g, at(l), :] = (sent[g, at(l), :].astype(f32) + got[g, at(l), :].astype(f32)).astype(bf)

                loop(local, add)

            rs_copy(a, g, sign).start()

    near = jnp.where(f < nf // 2, 1, -1)

    def rs_chain(a):
        def steps(t):
            for sign in (near, -near):
                rs_step(a, jnp.where(sign > 0, nf - 1 - t, t), sign)

        loop(nf - 1, steps)

    at_edge = (f == 0) | (f == nf - 1)

    w_pass(0)
    for n in range(nf):
        partial_sum(0, f_at(n + 1) if n < nf - 1 else f)
        if n < nf - 1:
            z_pass(1, order[n])

    @pl.when(at_edge)
    def _():
        rs_chain(0)

    w_pass(1)
    for n in range(nf):
        partial_sum(1, f_at(n + 1) if n < nf - 1 else f)

    @pl.when(jnp.logical_not(at_edge))
    def _():
        rs_chain(0)

    rs_chain(1)

    for a, got in enumerate((pre_r, prj_r)):
        for spot, edge in ((f, 0), (nf, nf - 1)):

            @pl.when(f == edge)
            def _():
                got[spot] = jnp.zeros(got.shape[1:], bf)

            @pl.when(f != edge)
            def _():
                with scope("wait_own"):
                    rs_wait(a, spot)

    def middle(l, carry):
        here = at(l)
        gate = own[here, :units] + pre_r[f, here, :units].astype(f32) + pre_r[nf, here, :units].astype(f32)
        up = own[here, units : 2 * units] + pre_r[f, here, units:].astype(f32) + pre_r[nf, here, units:].astype(f32)
        proj = own[here, 2 * units :] + prj_r[f, here, :].astype(f32) + prj_r[nf, here, :].astype(f32)
        zero, one = choose(f, (l * span).astype(f32), span)
        scale = jnp.sum(
            jnp.where(zero, codes(f, 2), 0.0) + jnp.where(one, codes(f, 3), 0.0), axis=1, keepdims=True
        )
        sig = jax.nn.sigmoid(gate)
        act = gate * sig
        hidden = act * up
        slot_gate = jnp.sum(hidden * proj, axis=1, keepdims=True)
        delta = scale * proj
        dl[l, group(f), :units] = (delta * up * sig * (1.0 + gate * (1.0 - sig))).astype(bf)
        dl[l, group(f), units : 2 * units] = (delta * act).astype(bf)
        dl[l, group(f), 2 * units :] = (scale * hidden).astype(bf)
        return (
            carry[0] + jnp.sum(jnp.where(zero, slot_gate, 0.0), axis=0, keepdims=True),
            carry[1] + jnp.sum(jnp.where(one, slot_gate, 0.0), axis=0, keepdims=True),
        )

    def ag_copy(h, g, sign, spot):
        held = dl.at[h * part : (h + 1) * part, group(g), :]
        return put(held, held, sa.at[h, spot], ra.at[h, g], (k, e, f + sign))

    def has(sign):
        return (f + sign >= 0) & (f + sign < nf)

    def ag_own(h):
        for sign, spot in ((1, f), (-1, nf)):

            @pl.when(has(sign))
            def _():
                ag_copy(h, f, sign, spot).start()

    def ag_step(h, t, sign):
        g = f - sign * t

        @pl.when((g >= 0) & (g < nf))
        def _():
            with scope("wait_ag"):
                ag_copy(h, g, sign, g).wait_recv()

            @pl.when(has(sign))
            def _():
                ag_copy(h, g, sign, g).start()

    nothing = jnp.zeros((1, ne * tcount), f32)
    parts = (nothing, nothing)
    for h in range(halves):
        with scope("middle"):
            parts = lax.fori_loop(h * part, (h + 1) * part, middle, parts)
        ag_own(h)

    for ee in range(ne):
        for j in range(2):
            gg_s[ee, j : j + 1, :] = parts[j][:, ee * tcount : (ee + 1) * tcount]

    def gg_copy(de):
        return put(gg_s.at[e_at(de)], gg_r.at[de], sg_sem.at[de], rg_sem.at[de], (k, e_at(de), f))

    for de in range(1, ne):
        gg_copy(de).start()

    for de in range(1, ne):
        for g in range(nf):
            y_whole(0, g, de, e).wait_send()

    def ret_copy(g, de):
        return put(
            tokb.at[g, mine(e_at(de)), :], ret_r.at[g, de], st.at[g, de], rt.at[g, de], (k, e_at(de), f)
        )

    def returned(g):
        with scope("returned"):

            def column(kk):
                for l in range(local):
                    sg[l * span : (l + 1) * span, :] = dot(
                        dl[l, group(g), : 2 * units], weights[l, cut(kk), : 2 * units], ((1,), (1,))
                    ).astype(bf)
                tokb[g, :, cut(kk)] = dot(place[g], sg[...], ((0,), (0,))).astype(bf)

            loop(nk, column)
        for de in range(1, ne):
            ret_copy(g, de).start()

    def final(g):
        with scope("final"):
            total = tokb[g, mine(e), :].astype(f32)
            for de in range(1, ne):
                with scope("wait_ret"):
                    put(ret_r.at[g, de], ret_r.at[g, de], st.at[g, de], rt.at[g, de], (k, e_at(de), f)).wait_recv()
                total += ret_r[g, de].astype(f32)
            tg_s[g] = total.astype(bf)
            d = lax.rem(g - f + nf, nf)
            for kk in range(nk):
                there = tg_ref.at[:, strip(kk, f)]

                @pl.when(d > 0)
                def _():
                    put(tg_s.at[g, :, cut(kk)], there, so.at[d], ro.at[d], (k, e, g)).start()

                @pl.when(d == 0)
                def _():
                    pltpu.make_async_copy(tg_s.at[g, :, cut(kk)], there, own_sems.at[3]).start()

    def both(t, work):
        def side(n):
            g = f - (1 - 2 * n) * t

            @pl.when((g >= 0) & (g < nf))
            def _():
                work(g)

        loop(2, side)

    def gradient(kk, l):
        ahead = dot(inp[l, :, cut(kk)], dl[l, :, : 2 * units], ((0,), (0,)))
        down = dot(ups[l, :, cut(kk)], dl[l, :, 2 * units :], ((0,), (0,)))
        return ahead, down

    def g1_copy(dx, l):
        return put(g1_out.at[dx, l], g1_in.at[dx, l], s1.at[dx, l], r1.at[dx, l], (partner, e, f))

    def g2_copy(dx, l):
        return put(g2_out.at[dx, l], g2_in.at[dx, l], s2.at[dx, l], r2.at[dx, l], (chip_at(dx, c), e, f))

    def to_core(h):
        def one(n):
            l = h * part + n
            for dx in [*range(1, chips), 0]:
                ahead, down = gradient(chip_at(dx, 1 - c), l)
                g1_out[dx, l, :, : 2 * units] = ahead.astype(bf)
                g1_out[dx, l, :, 2 * units :] = down.astype(bf)
                g1_copy(dx, l).start()

        with scope("to_core"):
            loop(part, one)

    def summed(dx, l):
        ahead, down = gradient(chip_at(dx, c), l)
        with scope("wait_g1"):
            g1_copy(dx, l).wait_recv()
        ahead += g1_in[dx, l, :, : 2 * units].astype(f32)
        down += g1_in[dx, l, :, 2 * units :].astype(f32)
        return ahead, down

    def to_chip(h):
        def one(n):
            l = h * part + n
            for dx in range(1, chips):
                ahead, down = summed(dx, l)
                g2_out[dx, l, :, : 2 * units] = ahead.astype(bf)
                g2_out[dx, l, :, 2 * units :] = down.astype(bf)
                g2_copy(dx, l).start()

        with scope("to_chip"):
            loop(part, one)

    def keep(l):
        ahead, down = summed(0, l)
        grad_ref[0, l] = ahead[:, :units]
        grad_ref[1, l] = ahead[:, units:]
        grad_ref[2, l] = down

    returned(f)
    for h in range(halves - 1):
        for t in range(1, nf):
            for sign in (1, -1):
                ag_step(h, t, sign)
        to_core(h)
    last = halves - 1
    for t in range(1, nf):
        for sign in (1, -1):
            ag_step(last, t, sign)
        if t == 1:
            for h in range(halves - 1):
                to_chip(h)
        if t == nf - 1:
            to_core(last)
            to_chip(last)
        both(t, returned)
        if t == 1:
            final(f)
        else:
            both(t - 1, final)
    both(nf - 1, final)
    with scope("keep"):
        loop(local, keep)

    total = [gg_s[e, j : j + 1, :] for j in range(2)]
    for de in range(1, ne):
        gg_copy(de).wait_recv()
        for j in range(2):
            total[j] += gg_r[de, j : j + 1, :]
    for j in range(2):
        gg_ref[j : j + 1, :] = total[j].astype(bf)

    def collect(l):
        for dx in range(1, chips):
            with scope("wait_g2"):
                g2_copy(dx, l).wait_recv()
            got = g2_in[dx, l].astype(f32)
            for n in range(3):
                grad_ref[n, l] += got[:, n * units : (n + 1) * units]

    loop(local, collect)

    for d in range(1, nf):
        with scope("wait_tg"):
            put(tg_s.at[0], tg_s.at[0], so.at[d], ro.at[d], (k, e, f_at(d))).wait()
    pltpu.make_async_copy(tg_s.at[0], tg_s.at[0], own_sems.at[3]).wait()

    for de in range(ne):
        for d in range(nf):
            if de or d:
                info_copy(de, d).wait_send()
    for d in range(1, nf):
        for a in range(2):
            z_whole(a, d).wait_send()
    for g in range(nf):

        @pl.when(f != g)
        def _():
            for a in range(2):
                rs_copy(a, g, 1).wait_send()

    for h in range(halves):
        for g in range(nf):
            sign = jnp.where(f >= g, 1, -1)

            @pl.when(has(sign))
            def _():
                ag_copy(h, g, sign, g).wait_send()

        @pl.when(f > 0)
        def _():
            ag_copy(h, f, -1, nf).wait_send()

    for de in range(1, ne):
        gg_copy(de).wait_send()
        for g in range(nf):
            y_whole(1, g, de, e).wait_send()
            ret_copy(g, de).wait_send()
    for dx in range(chips):
        for a in range(2):
            w_core(a, dx, k).wait_send()
            if dx:
                w_chip(a, dx, k).wait_send()

        def sent(l):
            g1_copy(dx, l).wait_send()
            if dx:
                g2_copy(dx, l).wait_send()

        loop(local, sent)


def per_device(mesh_shape, tokens, out_grad, expert_ids, gate_probs, params, moment_first, moment_second):
    nk, ne, nf = mesh_shape["cuts"], mesh_shape["exp"], mesh_shape["fsdp"]
    token_count, width = tokens.shape
    local, rows, units = params.shape[1:]
    cap = 10 * token_count // 32
    chips = nk // CORES
    span = ne * cap
    slots = local * span
    depth = nk * rows
    halves = 2 if local % 2 == 0 else 1
    bf, f32 = jnp.bfloat16, jnp.float32

    sizes = (nk, ne, nf, local, cap, token_count, rows, units)

    def vm(*shape, kind=bf):
        return pltpu.VMEM(shape, kind)

    def sem(*shape):
        return pltpu.SemaphoreType.DMA(shape)

    scratch = [
        vm(token_count, width),
        vm(token_count, width),
        vm(3, local, rows, units, kind=f32),
        vm(nf, ne, 8, token_count, kind=f32),
        vm(local, depth, 3 * units),
        vm(nf, ne * token_count, depth),
        vm(nf, ne * token_count, depth),
        vm(nf, slots, ne * token_count),
        vm(local, nf * span, depth),
        vm(local, nf * span, depth),
        vm(nf, slots, 2 * units),
        vm(nf, slots, units),
        vm(nf + 1, slots, 2 * units),
        vm(nf + 1, slots, units),
        vm(slots, 3 * units, kind=f32),
        vm(local, nf * span, 3 * units),
        vm(slots, rows),
        vm(nf, ne, token_count, depth),
        vm(nf, token_count, depth),
        vm(ne, 8, token_count, kind=f32),
        vm(ne, 8, token_count, kind=f32),
        vm(chips, local, rows, 3 * units),
        vm(chips, local, rows, 3 * units),
        vm(chips, local, rows, 3 * units),
        vm(chips, local, rows, 3 * units),
        sem(ne, nf), sem(ne, nf),
        sem(2, nf), sem(2, nf),
        sem(2, nf, ne), sem(2, nf, ne),
        sem(2, chips), sem(2, chips),
        sem(2, chips), sem(2, chips),
        sem(2, nf), sem(2, nf + 1),
        sem(halves, nf + 1), sem(halves, nf),
        sem(nf, ne), sem(nf, ne),
        sem(nf), sem(nf),
        sem(ne), sem(ne),
        sem(chips, local), sem(chips, local),
        sem(chips, local), sem(chips, local),
        sem(4),
    ]
    vmem = pl.BlockSpec(memory_space=pltpu.VMEM)
    hbm = pl.BlockSpec(memory_space=pl.ANY)
    token_grad, gates, gradient = pl.pallas_call(
        functools.partial(kernel, sizes),
        out_shape=(
            jax.ShapeDtypeStruct((token_count, width), bf),
            jax.ShapeDtypeStruct((2, token_count), bf),
            jax.ShapeDtypeStruct((3, local, rows, units), f32),
        ),
        in_specs=[vmem, vmem, hbm, hbm, hbm],
        out_specs=(hbm, vmem, vmem),
        scratch_shapes=scratch,
        compiler_params=pltpu.CompilerParams(
            collective_id=0, has_side_effects=True, vmem_limit_bytes=67043328
        ),
    )(expert_ids.T, gate_probs.T, tokens, out_grad, params)
    new_params, new_first, new_second = adam_update(params, gradient, moment_first, moment_second)
    return (token_grad, gates.T, new_params, new_first, new_second)


def solution(mesh):
    tokens_spec = P(("cuts", "exp", "fsdp"), None)
    weights_spec = P(None, "exp", ("cuts", "fsdp"), None)
    return jax.shard_map(
        functools.partial(per_device, dict(mesh.shape)),
        mesh=mesh,
        in_specs=(tokens_spec,) * 4 + (weights_spec,) * 3,
        out_specs=(tokens_spec,) * 2 + (weights_spec,) * 3,
        check_vma=False,
    )
```

time: 221 us -> 174 us (0.79)
  Pallas kernels: 202 us -> 163 us
  other arithmetic: 14.7 us -> 8 us
    pallas_call x1, Pallas kernels: 202 us -> 163 us  [per_device(): pl.pallas_call(functools.partial(kernel, sizes), out_shape=(jax.ShapeDtyp...]
    convert_element_type x4 -> x0, other arithmetic: 3.43 us -> none  [the longest x1 2.06 us: per_device(): weights = params.astype(bf)]
where the time goes in v2:
time: 174 us; the launch traced here: 173 us
  Pallas kernels  163 us (94%)
  other arithmetic  8 us (5%)
    pallas_call x1, Pallas kernels, per_device(): pl.pallas_call(functools.partial(kernel, sizes), out_shape=(jax.ShapeDtyp...  163 us
    sub x1, other arithmetic, adam_update(): new_params = params - learn_rate * (stepped + weight_decay * params)  8 us

profile of v2, /device:TPU:0, one launch (start us, length us, event | category | flops | bytes accessed | tf_op | source)
XLA Modules:
  0.0 173.3 jit_solution(4695976375510850049)
XLA Ops:
  0.6 163.2 %shard_map.110 = (bf16[128,4096]{1,0:T(8,128)(2,1)}, bf16[2,128]{1,0:T(2,128)(2,1)}, f32[3,4,256,256]{3,2,1,0:T(8,128)}) custom-call(s32[2,128]{1,0:T(2,128)} %bitcast.3, bf16[2,128]{1,0:T(2,128)(2,1)} %bitcast.4, bf16[128,4096]{1,0:T(8,128)(2,1)} %tok_hbm.1, bf16[128,4096]{1,0:T(8,128)(2,1)} %og_hbm.1, f32[3,4,256,256]{3,2,1,0:T(8,128)} %params_hbm.1), custom_call_target="tpu_custom_call" | custom-call | tf_op jit(solution)/shard_map/pallas_call | solution.py:647
  163.8 0.0 copy-start
  163.8 0.0 copy-start.1
  163.9 8.0 %multiply_subtract_fusion = (f32[3,4,256,256]{3,2,1,0:T(8,128)}, f32[3,4,256,256]{3,2,1,0:T(8,128)}, f32[3,4,256,256]{3,2,1,0:T(8,128)}) fusion(f32[3,4,256,256]{3,2,1,0:T(8,128)} %params_hbm.1, f32[3,4,256,256]{3,2,1,0:T(8,128)} %get-tuple-element.10, f32[3,4,256,256]{3,2,1,0:T(8,128)} %param.12, f32[3,4,256,256]{3,2,1,0:T(8,128)} %param.13), kind=kLoop, calls=%fused_computation.2 | loop fusion | flops 11796480 | bytes 22020096 | tf_op jit(solution)/shard_map/sub | solution.py:26
  171.9 0.0 copy-done
  171.9 1.0 copy.14
  172.8 0.0 copy-done.1
  172.8 0.5 copy.15
Async XLA Ops:
  163.8 8.0 %copy-start = (bf16[128,4096]{1,0:T(8,128)(2,1)S(1)}, bf16[128,4096]{1,0:T(8,128)(2,1)}, u32[]{:S(2)}) copy-start(bf16[128,4096]{1,0:T(8,128)(2,1)} %get-tuple-element.19) | copy-start | bytes 3145732
  163.8 9.0 %copy-start.1 = (bf16[2,128]{1,0:T(2,128)(2,1)S(1)}, bf16[2,128]{1,0:T(2,128)(2,1)}, u32[]{:S(2)}) copy-start(bf16[2,128]{1,0:T(2,128)(2,1)} %get-tuple-element.9) | copy-start | bytes 1540

commit v3 on v2

--- a/solution.py
+++ b/solution.py
@@ -43,7 +43,7 @@
     sizes,
     ids_ref, gates_ref, tok_hbm, og_hbm, params_hbm,
     tg_ref, gg_ref, grad_ref,
-    tok_ref, og_ref, par_ref, info, weights, tokb, ogb, place, inp, ups, pre_s, prj_s, pre_r, prj_r, own, dl, sg,
+    tok_ref, og_ref, info, weights, tokb, ogb, place, inp, ups, pre_s, prj_s, pre_r, prj_r, own, dl, sg,
     ret_r, tg_s, gg_s, gg_r, g1_out, g1_in, g2_out, g2_in,
     si, ri, sz, rz, sy, ry, sw, rw, sv, rv, sp, rp, sa, ra, st, rt, so, ro, sg_sem, rg_sem, s1, r1, s2, r2,
     own_sems,
@@ -52,8 +52,6 @@
     chips = nk // CORES
     span = ne * cap
     slots = local * span
-    halves = 2 if local % 2 == 0 else 1
-    part = local // halves
     bf = jnp.bfloat16
     f32 = jnp.float32
     k, e, f = lax.axis_index("cuts"), lax.axis_index("exp"), lax.axis_index("fsdp")
@@ -101,7 +99,7 @@
         pl.semaphore_signal(barrier, inc=1, device_id=(chip_at(dx, c), e, f), device_id_type=MESH)
         partners += 1
 
-    staged = ((tok_hbm, tok_ref), (og_hbm, og_ref), (params_hbm, par_ref))
+    staged = ((tok_hbm, tok_ref), (og_hbm, og_ref), (params_hbm, grad_ref))
     for n, (src, dst) in enumerate(staged):
         pltpu.make_async_copy(src, dst, own_sems.at[n]).start()
 
@@ -118,10 +116,10 @@
         info[f, e, j : j + 1, :] = (ids_ref[j : j + 1, :] * span + e * cap).astype(f32) + position
         info[f, e, j + 2 : j + 3, :] = gates_ref[j : j + 1, :].astype(f32)
 
-    pltpu.make_async_copy(params_hbm, par_ref, own_sems.at[2]).wait()
+    pltpu.make_async_copy(params_hbm, grad_ref, own_sems.at[2]).wait()
     for l in range(local):
         for n in range(3):
-            weights[l, cut(k), n * units : (n + 1) * units] = par_ref[n, l].astype(bf)
+            weights[l, cut(k), n * units : (n + 1) * units] = grad_ref[n, l].astype(bf)
     for n, (src, dst) in enumerate(staged[:2]):
         pltpu.make_async_copy(src, dst, own_sems.at[n]).wait()
     with scope("barrier"):
@@ -131,16 +129,22 @@
         mark = info.at[f, e]
         return put(mark, mark, si.at[de, d], ri.at[de, d], (k, e_at(de), f_at(d)))
 
-    order = sorted(range(1, nf), key=lambda d: -min(d, nf - d))
     arrays = ((tok_ref, tokb), (og_ref, ogb))
     wide = (pl.ds(0, 2 * units), pl.ds(2 * units, units))
 
-    def z_start(a, d):
+    def sides(t, work):
+        for sign in (1, -1):
+            g = f + sign * t
+
+            @pl.when((g >= 0) & (g < nf))
+            def _():
+                work(g)
+
+    def z_start(a, g):
         src, dst = arrays[a]
         for kk in range(nk):
             put(
-                src.at[:, strip(kk, f_at(d))], dst.at[f, mine(e), cut(kk)], sz.at[a, d], rz.at[a, d],
-                (k, e, f_at(d)),
+                src.at[:, strip(kk, g)], dst.at[f, mine(e), cut(kk)], sz.at[a, g], rz.at[a, f], (k, e, g)
             ).start()
 
     def y_own_start(a):
@@ -163,40 +167,40 @@
     def whole(dst, g, ee, send, recv, device):
         return put(dst.at[g, mine(ee), :], dst.at[g, mine(ee), :], send, recv, device)
 
-    def z_whole(a, d):
-        return whole(arrays[a][1], f_at(nf - d), e, sz.at[a, d], rz.at[a, d], (k, e, f_at(d)))
+    def z_whole(a, g):
+        return whole(arrays[a][1], g, e, sz.at[a, g], rz.at[a, g], (k, e, g))
 
     def y_whole(a, g, de, ee):
         return whole(arrays[a][1], g, ee, sy.at[a, g, de], ry.at[a, g, de], (k, e_at(de), f))
 
-    def z_pass(a, d):
+    def z_pass(a, g):
         with scope("wait_z"):
-            z_whole(a, d).wait_recv()
+            z_whole(a, g).wait_recv()
         for de in range(1, ne):
-            y_whole(a, f_at(nf - d), de, e).start()
+            y_whole(a, g, de, e).start()
 
     for de in range(ne):
         for d in range(nf):
             if de or d:
                 info_copy(de, d).start()
-    for d in order:
-        z_start(0, d)
+    for t in range(1, nf):
+        sides(t, functools.partial(z_start, 0))
     y_own_start(0)
     for a in range(2):
         for dx in range(1, chips):
             w_chip(a, dx, k).start()
         w_core(a, 0, k).start()
         if a == 0:
-            for d in order:
-                z_start(1, d)
+            for t in range(1, nf):
+                sides(t, functools.partial(z_start, 1))
 
     for src, dst in arrays:
         for kk in range(nk):
             dst[f, mine(e), cut(kk)] = src[:, strip(kk, f)]
 
-    for n, d in enumerate(order):
-        z_pass(0, d)
-        if n == 0:
+    for t in range(1, nf):
+        sides(t, functools.partial(z_pass, 0))
+        if t == 1:
             y_own_start(1)
     for de in range(ne):
         for d in range(nf):
@@ -209,6 +213,9 @@
                 owner = chip_at(chips - dx, c)
                 w_chip(a, dx, owner).wait_recv()
                 w_core(a, dx, owner).start()
+
+    def w_done(a):
+        with scope("wait_w2"):
             for dx in range(chips):
                 w_core(a, dx, chip_at(chips - dx, 1 - c)).wait_recv()
 
@@ -247,8 +254,11 @@
 
             def expert(l):
                 out = dot(rows_of[l, group(g), :], weights[l, :, wide[a]], ((1,), (0,)))
-                own[at(l), wide[a]] = out
                 sums[g, at(l), :] = out.astype(bf)
+
+                @pl.when(g == f)
+                def _():
+                    own[at(l), wide[a]] = out
 
             loop(local, expert)
 
@@ -281,32 +291,55 @@
 
     near = jnp.where(f < nf // 2, 1, -1)
 
-    def rs_chain(a):
-        def steps(t):
+    def rs_chain(a, first=0):
+        def steps(n):
+            t = n + first
             for sign in (near, -near):
                 rs_step(a, jnp.where(sign > 0, nf - 1 - t, t), sign)
 
-        loop(nf - 1, steps)
+        loop(nf - 1 - first, steps)
 
     at_edge = (f == 0) | (f == nf - 1)
 
+    def both(t, work):
+        def side(n):
+            g = f + (1 - 2 * n) * t
+
+            @pl.when((g >= 0) & (g < nf))
+            def _():
+                work(g)
+
+        loop(2, side)
+
     w_pass(0)
-    for n in range(nf):
-        partial_sum(0, f_at(n + 1) if n < nf - 1 else f)
-        if n < nf - 1:
-            z_pass(1, order[n])
+    w_done(0)
+    partial_sum(0, f)
+    for t in range(1, nf):
+        both(t, functools.partial(partial_sum, 0))
+        if t == min(2, nf - 1):
+            sides(1, functools.partial(z_pass, 1))
 
     @pl.when(at_edge)
     def _():
         rs_chain(0)
 
     w_pass(1)
-    for n in range(nf):
-        partial_sum(1, f_at(n + 1) if n < nf - 1 else f)
+    for t in range(2, nf):
+        sides(t, functools.partial(z_pass, 1))
+    w_done(1)
 
     @pl.when(jnp.logical_not(at_edge))
     def _():
-        rs_chain(0)
+        rs_step(0, jnp.where(near > 0, nf - 1, 0), near)
+
+    partial_sum(1, f)
+    for t in range(1, nf):
+        both(t, functools.partial(partial_sum, 1))
+
+    @pl.when(jnp.logical_not(at_edge))
+    def _():
+        rs_step(0, jnp.where(near > 0, 0, nf - 1), -near)
+        rs_chain(0, 1)
 
     rs_chain(1)
 
@@ -345,7 +378,7 @@
         )
 
     def ag_copy(h, g, sign, spot):
-        held = dl.at[h * part : (h + 1) * part, group(g), :]
+        held = dl.at[h, group(g), :]
         return put(held, held, sa.at[h, spot], ra.at[h, g], (k, e, f + sign))
 
     def has(sign):
@@ -372,10 +405,12 @@
 
     nothing = jnp.zeros((1, ne * tcount), f32)
     parts = (nothing, nothing)
-    for h in range(halves):
+    ahead = 2
+    for h in range(local):
         with scope("middle"):
-            parts = lax.fori_loop(h * part, (h + 1) * part, middle, parts)
-        ag_own(h)
+            parts = middle(jnp.int32(h), parts)
+        if h < ahead:
+            ag_own(h)
 
     for ee in range(ne):
         for j in range(2):
@@ -391,35 +426,37 @@
         for g in range(nf):
             y_whole(0, g, de, e).wait_send()
 
-    def ret_copy(g, de):
+    def ret_copy(g, de, kk):
         return put(
-            tokb.at[g, mine(e_at(de)), :], ret_r.at[g, de], st.at[g, de], rt.at[g, de], (k, e_at(de), f)
+            tokb.at[g, mine(e_at(de)), cut(kk)], ret_r.at[g, de - 1, :, cut(kk)], st.at[g, de, kk],
+            rt.at[g, de, kk], (k, e_at(de), f),
         )
+
+    def slot_rows(l, g):
+        with scope("slot_rows"):
+            sg[g, at(l), :] = dot(dl[l, group(g), : 2 * units], weights[l, :, : 2 * units], ((1,), (1,))).astype(bf)
 
     def returned(g):
         with scope("returned"):
 
             def column(kk):
-                for l in range(local):
-                    sg[l * span : (l + 1) * span, :] = dot(
-                        dl[l, group(g), : 2 * units], weights[l, cut(kk), : 2 * units], ((1,), (1,))
-                    ).astype(bf)
-                tokb[g, :, cut(kk)] = dot(place[g], sg[...], ((0,), (0,))).astype(bf)
+                tokb[g, :, cut(kk)] = dot(place[g], sg[g, :, cut(kk)], ((0,), (0,))).astype(bf)
+                for de in range(1, ne):
+                    ret_copy(g, de, kk).start()
 
             loop(nk, column)
-        for de in range(1, ne):
-            ret_copy(g, de).start()
 
     def final(g):
         with scope("final"):
-            total = tokb[g, mine(e), :].astype(f32)
-            for de in range(1, ne):
-                with scope("wait_ret"):
-                    put(ret_r.at[g, de], ret_r.at[g, de], st.at[g, de], rt.at[g, de], (k, e_at(de), f)).wait_recv()
-                total += ret_r[g, de].astype(f32)
-            tg_s[g] = total.astype(bf)
             d = lax.rem(g - f + nf, nf)
-            for kk in range(nk):
+
+            def column(kk):
+                total = tokb[g, mine(e), cut(kk)].astype(f32)
+                for de in range(1, ne):
+                    with scope("wait_ret"):
+                        ret_copy(g, de, kk).wait_recv()
+                    total += ret_r[g, de - 1, :, cut(kk)].astype(f32)
+                tg_s[g, :, cut(kk)] = total.astype(bf)
                 there = tg_ref.at[:, strip(kk, f)]
 
                 @pl.when(d > 0)
@@ -430,15 +467,7 @@
                 def _():
                     pltpu.make_async_copy(tg_s.at[g, :, cut(kk)], there, own_sems.at[3]).start()
 
-    def both(t, work):
-        def side(n):
-            g = f - (1 - 2 * n) * t
-
-            @pl.when((g >= 0) & (g < nf))
-            def _():
-                work(g)
-
-        loop(2, side)
+            loop(nk, column)
 
     def gradient(kk, l):
         ahead = dot(inp[l, :, cut(kk)], dl[l, :, : 2 * units], ((0,), (0,)))
@@ -449,19 +478,15 @@
         return put(g1_out.at[dx, l], g1_in.at[dx, l], s1.at[dx, l], r1.at[dx, l], (partner, e, f))
 
     def g2_copy(dx, l):
-        return put(g2_out.at[dx, l], g2_in.at[dx, l], s2.at[dx, l], r2.at[dx, l], (chip_at(dx, c), e, f))
-
-    def to_core(h):
-        def one(n):
-            l = h * part + n
+        return put(g2_out.at[dx - 1, l], g2_in.at[dx - 1, l], s2.at[dx, l], r2.at[dx, l], (chip_at(dx, c), e, f))
+
+    def to_core(l):
+        with scope("to_core"):
             for dx in [*range(1, chips), 0]:
                 ahead, down = gradient(chip_at(dx, 1 - c), l)
                 g1_out[dx, l, :, : 2 * units] = ahead.astype(bf)
                 g1_out[dx, l, :, 2 * units :] = down.astype(bf)
                 g1_copy(dx, l).start()
-
-        with scope("to_core"):
-            loop(part, one)
 
     def summed(dx, l):
         ahead, down = gradient(chip_at(dx, c), l)
@@ -471,17 +496,13 @@
         down += g1_in[dx, l, :, 2 * units :].astype(f32)
         return ahead, down
 
-    def to_chip(h):
-        def one(n):
-            l = h * part + n
+    def to_chip(l):
+        with scope("to_chip"):
             for dx in range(1, chips):
                 ahead, down = summed(dx, l)
-                g2_out[dx, l, :, : 2 * units] = ahead.astype(bf)
-                g2_out[dx, l, :, 2 * units :] = down.astype(bf)
+                g2_out[dx - 1, l, :, : 2 * units] = ahead.astype(bf)
+                g2_out[dx - 1, l, :, 2 * units :] = down.astype(bf)
                 g2_copy(dx, l).start()
-
-        with scope("to_chip"):
-            loop(part, one)
 
     def keep(l):
         ahead, down = summed(0, l)
@@ -489,28 +510,37 @@
         grad_ref[1, l] = ahead[:, units:]
         grad_ref[2, l] = down
 
-    returned(f)
-    for h in range(halves - 1):
+    last = local - 1
+    for l in range(local):
         for t in range(1, nf):
             for sign in (1, -1):
-                ag_step(h, t, sign)
-        to_core(h)
-    last = halves - 1
-    for t in range(1, nf):
-        for sign in (1, -1):
-            ag_step(last, t, sign)
-        if t == 1:
-            for h in range(halves - 1):
-                to_chip(h)
-        if t == nf - 1:
-            to_core(last)
-            to_chip(last)
-        both(t, returned)
-        if t == 1:
-            final(f)
-        else:
-            both(t - 1, final)
-    both(nf - 1, final)
+                ag_step(l, t, sign)
+            if t == 1 and l + ahead < local:
+                ag_own(l + ahead)
+            if t == nf - 1:
+                to_core(jnp.int32(l))
+            if t == 1:
+                slot_rows(jnp.int32(l), f)
+                if l == last:
+                    returned(f)
+            if l < last:
+                if t == 2 and l:
+                    to_chip(jnp.int32(l - 1))
+                if t == nf - 1:
+                    for near_t in range(1, nf):
+                        both(near_t, functools.partial(slot_rows, jnp.int32(l)))
+            else:
+                both(t, functools.partial(slot_rows, jnp.int32(l)))
+                both(t, returned)
+                if t == 1 and l:
+                    to_chip(jnp.int32(l - 1))
+                if t == 2:
+                    final(f)
+                if t > 2:
+                    both(t - 2, final)
+    to_chip(jnp.int32(last))
+    for t in range(max(1, nf - 2), nf):
+        both(t, final)
     with scope("keep"):
         loop(local, keep)
 
@@ -526,7 +556,7 @@
         for dx in range(1, chips):
             with scope("wait_g2"):
                 g2_copy(dx, l).wait_recv()
-            got = g2_in[dx, l].astype(f32)
+            got = g2_in[dx - 1, l].astype(f32)
             for n in range(3):
                 grad_ref[n, l] += got[:, n * units : (n + 1) * units]
 
@@ -541,17 +571,15 @@
         for d in range(nf):
             if de or d:
                 info_copy(de, d).wait_send()
-    for d in range(1, nf):
-        for a in range(2):
-            z_whole(a, d).wait_send()
     for g in range(nf):
 
         @pl.when(f != g)
         def _():
             for a in range(2):
+                z_whole(a, g).wait_send()
                 rs_copy(a, g, 1).wait_send()
 
-    for h in range(halves):
+    for h in range(local):
         for g in range(nf):
             sign = jnp.where(f >= g, 1, -1)
 
@@ -567,7 +595,8 @@
         gg_copy(de).wait_send()
         for g in range(nf):
             y_whole(1, g, de, e).wait_send()
-            ret_copy(g, de).wait_send()
+            for kk in range(nk):
+                ret_copy(g, de, kk).wait_send()
     for dx in range(chips):
         for a in range(2):
             w_core(a, dx, k).wait_send()
@@ -591,7 +620,6 @@
     span = ne * cap
     slots = local * span
     depth = nk * rows
-    halves = 2 if local % 2 == 0 else 1
     bf, f32 = jnp.bfloat16, jnp.float32
 
     sizes = (nk, ne, nf, local, cap, token_count, rows, units)
@@ -605,7 +633,6 @@
     scratch = [
         vm(token_count, width),
         vm(token_count, width),
-        vm(3, local, rows, units, kind=f32),
         vm(nf, ne, 8, token_count, kind=f32),
         vm(local, depth, 3 * units),
         vm(nf, ne * token_count, depth),
@@ -619,23 +646,23 @@
         vm(nf + 1, slots, units),
         vm(slots, 3 * units, kind=f32),
         vm(local, nf * span, 3 * units),
-        vm(slots, rows),
-        vm(nf, ne, token_count, depth),
+        vm(nf, slots, depth),
+        vm(nf, ne - 1, token_count, depth),
         vm(nf, token_count, depth),
         vm(ne, 8, token_count, kind=f32),
         vm(ne, 8, token_count, kind=f32),
         vm(chips, local, rows, 3 * units),
         vm(chips, local, rows, 3 * units),
-        vm(chips, local, rows, 3 * units),
-        vm(chips, local, rows, 3 * units),
+        vm(chips - 1, local, rows, 3 * units),
+        vm(chips - 1, local, rows, 3 * units),
         sem(ne, nf), sem(ne, nf),
         sem(2, nf), sem(2, nf),
         sem(2, nf, ne), sem(2, nf, ne),
         sem(2, chips), sem(2, chips),
         sem(2, chips), sem(2, chips),
         sem(2, nf), sem(2, nf + 1),
-        sem(halves, nf + 1), sem(halves, nf),
-        sem(nf, ne), sem(nf, ne),
+        sem(local, nf + 1), sem(local, nf),
+        sem(nf, ne, nk), sem(nf, ne, nk),
         sem(nf), sem(nf),
         sem(ne), sem(ne),
         sem(chips, local), sem(chips, local),

time: 174 us -> 168 us (0.966)
  Pallas kernels: 163 us -> 158 us
    pallas_call x1, Pallas kernels: 163 us -> 158 us  [per_device(): pl.pallas_call(functools.partial(kernel, sizes), out_shape=(jax.ShapeDtyp...]
where the time goes in v3:
time: 168 us
  Pallas kernels  158 us (94%)
  other arithmetic  8 us (5%)
    pallas_call x1, Pallas kernels, per_device(): pl.pallas_call(functools.partial(kernel, sizes), out_shape=(jax.ShapeDtyp...  158 us
    sub x1, other arithmetic, adam_update(): new_params = params - learn_rate * (stepped + weight_decay * params)  8 us

profile of v3, /device:TPU:0, one launch (start us, length us, event | category | flops | bytes accessed | tf_op | source)
XLA Modules:
  0.0 168.0 jit_solution(16296507692200197097)
XLA Ops:
  0.6 157.8 %shard_map.110 = (bf16[128,4096]{1,0:T(8,128)(2,1)}, bf16[2,128]{1,0:T(2,128)(2,1)}, f32[3,4,256,256]{3,2,1,0:T(8,128)}) custom-call(s32[2,128]{1,0:T(2,128)} %bitcast.3, bf16[2,128]{1,0:T(2,128)(2,1)} %bitcast.4, bf16[128,4096]{1,0:T(8,128)(2,1)} %tok_hbm.1, bf16[128,4096]{1,0:T(8,128)(2,1)} %og_hbm.1, f32[3,4,256,256]{3,2,1,0:T(8,128)} %params_hbm.1), custom_call_target="tpu_custom_call" | custom-call | tf_op jit(solution)/shard_map/pallas_call | solution.py:674
  158.5 0.0 copy-start
  158.5 0.0 copy-start.1
  158.5 8.0 %multiply_subtract_fusion = (f32[3,4,256,256]{3,2,1,0:T(8,128)}, f32[3,4,256,256]{3,2,1,0:T(8,128)}, f32[3,4,256,256]{3,2,1,0:T(8,128)}) fusion(f32[3,4,256,256]{3,2,1,0:T(8,128)} %params_hbm.1, f32[3,4,256,256]{3,2,1,0:T(8,128)} %get-tuple-element.10, f32[3,4,256,256]{3,2,1,0:T(8,128)} %param.12, f32[3,4,256,256]{3,2,1,0:T(8,128)} %param.13), kind=kLoop, calls=%fused_computation.2 | loop fusion | flops 11796480 | bytes 22020096 | tf_op jit(solution)/shard_map/sub | solution.py:26
  166.5 0.0 copy-done
  166.5 1.0 copy.14
  167.5 0.0 copy-done.1
  167.5 0.5 copy.15
Async XLA Ops:
  158.5 8.0 %copy-start = (bf16[128,4096]{1,0:T(8,128)(2,1)S(1)}, bf16[128,4096]{1,0:T(8,128)(2,1)}, u32[]{:S(2)}) copy-start(bf16[128,4096]{1,0:T(8,128)(2,1)} %get-tuple-element.19) | copy-start | bytes 3145732
  158.5 9.0 %copy-start.1 = (bf16[2,128]{1,0:T(2,128)(2,1)S(1)}, bf16[2,128]{1,0:T(2,128)(2,1)}, u32[]{:S(2)}) copy-start(bf16[2,128]{1,0:T(2,128)(2,1)} %get-tuple-element.9) | copy-start | bytes 1540

commit v4 on v3

--- a/solution.py
+++ b/solution.py
@@ -1,4 +1,5 @@
 import functools
+import math
 
 import jax
 import jax.numpy as jnp
@@ -8,6 +9,8 @@
 from jax.sharding import PartitionSpec as P
 
 CORES = 2
+VMEM_ALL = 67043328
+MARGIN = 2 * 1024 * 1024
 MESH = pl.DeviceIdType.MESH
 
 decay_first = 0.9
@@ -41,9 +44,9 @@
 
 def kernel(
     sizes,
-    ids_ref, gates_ref, tok_hbm, og_hbm, params_hbm,
-    tg_ref, gg_ref, grad_ref,
-    tok_ref, og_ref, info, weights, tokb, ogb, place, inp, ups, pre_s, prj_s, pre_r, prj_r, own, dl, sg,
+    ids_ref, gates_ref, tok_ref, og_ref, params_hbm, first_hbm, second_hbm,
+    tg_ref, gg_ref, grad_ref, par_ref, first_ref, second_ref,
+    info, weights, tokb, ogb, place, inp, ups, pre_s, prj_s, pre_r, prj_r, own, dl, sg,
     ret_r, tg_s, gg_s, gg_r, g1_out, g1_in, g2_out, g2_in,
     si, ri, sz, rz, sy, ry, sw, rw, sv, rv, sp, rp, sa, ra, st, rt, so, ro, sg_sem, rg_sem, s1, r1, s2, r2,
     own_sems,
@@ -99,9 +102,9 @@
         pl.semaphore_signal(barrier, inc=1, device_id=(chip_at(dx, c), e, f), device_id_type=MESH)
         partners += 1
 
-    staged = ((tok_hbm, tok_ref), (og_hbm, og_ref), (params_hbm, grad_ref))
-    for n, (src, dst) in enumerate(staged):
-        pltpu.make_async_copy(src, dst, own_sems.at[n]).start()
+    staged = ((params_hbm, par_ref), (first_hbm, first_ref), (second_hbm, second_ref))
+    copies = [pltpu.make_async_copy(src, dst, own_sems.at[n]) for n, (src, dst) in enumerate(staged)]
+    copies[0].start()
 
     def iota(shape, dim):
         return lax.broadcasted_iota(jnp.int32, shape, dim)
@@ -116,18 +119,21 @@
         info[f, e, j : j + 1, :] = (ids_ref[j : j + 1, :] * span + e * cap).astype(f32) + position
         info[f, e, j + 2 : j + 3, :] = gates_ref[j : j + 1, :].astype(f32)
 
-    pltpu.make_async_copy(params_hbm, grad_ref, own_sems.at[2]).wait()
+    copies[0].wait()
     for l in range(local):
         for n in range(3):
-            weights[l, cut(k), n * units : (n + 1) * units] = grad_ref[n, l].astype(bf)
-    for n, (src, dst) in enumerate(staged[:2]):
-        pltpu.make_async_copy(src, dst, own_sems.at[n]).wait()
+            weights[l, cut(k), n * units : (n + 1) * units] = par_ref[n, l].astype(bf)
     with scope("barrier"):
         pl.semaphore_wait(barrier, partners)
 
     def info_copy(de, d):
         mark = info.at[f, e]
         return put(mark, mark, si.at[de, d], ri.at[de, d], (k, e_at(de), f_at(d)))
+
+    at_edge = (f == 0) | (f == nf - 1)
+
+    def far(n):
+        return jnp.where(at_edge, nf + 1 - n, n) if n > 1 else 1
 
     arrays = ((tok_ref, tokb), (og_ref, ogb))
     wide = (pl.ds(0, 2 * units), pl.ds(2 * units, units))
@@ -184,7 +190,7 @@
             if de or d:
                 info_copy(de, d).start()
     for t in range(1, nf):
-        sides(t, functools.partial(z_start, 0))
+        sides(far(t), functools.partial(z_start, 0))
     y_own_start(0)
     for a in range(2):
         for dx in range(1, chips):
@@ -192,14 +198,16 @@
         w_core(a, 0, k).start()
         if a == 0:
             for t in range(1, nf):
-                sides(t, functools.partial(z_start, 1))
-
+                sides(far(t), functools.partial(z_start, 1))
+
+    copies[1].start()
+    copies[2].start()
     for src, dst in arrays:
         for kk in range(nk):
             dst[f, mine(e), cut(kk)] = src[:, strip(kk, f)]
 
     for t in range(1, nf):
-        sides(t, functools.partial(z_pass, 0))
+        sides(far(t), functools.partial(z_pass, 0))
         if t == 1:
             y_own_start(1)
     for de in range(ne):
@@ -299,8 +307,6 @@
 
         loop(nf - 1 - first, steps)
 
-    at_edge = (f == 0) | (f == nf - 1)
-
     def both(t, work):
         def side(n):
             g = f + (1 - 2 * n) * t
@@ -315,7 +321,7 @@
     w_done(0)
     partial_sum(0, f)
     for t in range(1, nf):
-        both(t, functools.partial(partial_sum, 0))
+        both(far(t), functools.partial(partial_sum, 0))
         if t == min(2, nf - 1):
             sides(1, functools.partial(z_pass, 1))
 
@@ -325,7 +331,7 @@
 
     w_pass(1)
     for t in range(2, nf):
-        sides(t, functools.partial(z_pass, 1))
+        sides(far(t), functools.partial(z_pass, 1))
     w_done(1)
 
     @pl.when(jnp.logical_not(at_edge))
@@ -334,11 +340,15 @@
 
     partial_sum(1, f)
     for t in range(1, nf):
-        both(t, functools.partial(partial_sum, 1))
+        both(far(t), functools.partial(partial_sum, 1))
+        if t == 1:
+
+            @pl.when(jnp.logical_not(at_edge))
+            def _():
+                rs_step(0, jnp.where(near > 0, 0, nf - 1), -near)
 
     @pl.when(jnp.logical_not(at_edge))
     def _():
-        rs_step(0, jnp.where(near > 0, 0, nf - 1), -near)
         rs_chain(0, 1)
 
     rs_chain(1)
@@ -510,39 +520,62 @@
         grad_ref[1, l] = ahead[:, units:]
         grad_ref[2, l] = down
 
-    last = local - 1
-    for l in range(local):
+    def collect(l):
+        for dx in range(1, chips):
+            with scope("wait_g2"):
+                g2_copy(dx, l).wait_recv()
+            got = g2_in[dx - 1, l].astype(f32)
+            for n in range(3):
+                grad_ref[n, l] += got[:, n * units : (n + 1) * units]
+
+    def own_rows(l):
+        slot_rows(l, f)
+
+    loop(local, own_rows)
+    returned(f)
+    tail = min(2, local)
+    head = local - tail
+    for l in range(head):
         for t in range(1, nf):
             for sign in (1, -1):
                 ag_step(l, t, sign)
             if t == 1 and l + ahead < local:
                 ag_own(l + ahead)
-            if t == nf - 1:
+            if t == 2 and l:
+                to_chip(jnp.int32(l - 1))
+        to_core(jnp.int32(l))
+        for t in range(1, nf):
+            both(t, functools.partial(slot_rows, jnp.int32(l)))
+        if l == 0:
+            final(f)
+        else:
+            keep(jnp.int32(l - 1))
+    for t in range(1, nf):
+        for l in range(head, local):
+            for sign in (1, -1):
+                ag_step(l, t, sign)
+        if t == 1 and head:
+            to_chip(jnp.int32(head - 1))
+        if t == nf - 1:
+            for l in range(head, local):
                 to_core(jnp.int32(l))
-            if t == 1:
-                slot_rows(jnp.int32(l), f)
-                if l == last:
-                    returned(f)
-            if l < last:
-                if t == 2 and l:
-                    to_chip(jnp.int32(l - 1))
-                if t == nf - 1:
-                    for near_t in range(1, nf):
-                        both(near_t, functools.partial(slot_rows, jnp.int32(l)))
-            else:
-                both(t, functools.partial(slot_rows, jnp.int32(l)))
-                both(t, returned)
-                if t == 1 and l:
-                    to_chip(jnp.int32(l - 1))
-                if t == 2:
-                    final(f)
-                if t > 2:
-                    both(t - 2, final)
-    to_chip(jnp.int32(last))
-    for t in range(max(1, nf - 2), nf):
-        both(t, final)
+
+        def rows_back(g):
+            for l in range(head, local):
+                slot_rows(jnp.int32(l), g)
+            returned(g)
+
+        both(t, rows_back)
+    if not head:
+        final(f)
+    for n in range(max(tail, nf - 1)):
+        if n < tail:
+            to_chip(jnp.int32(head + n))
+        if n < nf - 1:
+            both(n + 1, final)
     with scope("keep"):
-        loop(local, keep)
+        for l in range(max(head - 1, 0), local):
+            keep(jnp.int32(l))
 
     total = [gg_s[e, j : j + 1, :] for j in range(2)]
     for de in range(1, ne):
@@ -552,20 +585,14 @@
     for j in range(2):
         gg_ref[j : j + 1, :] = total[j].astype(bf)
 
-    def collect(l):
-        for dx in range(1, chips):
-            with scope("wait_g2"):
-                g2_copy(dx, l).wait_recv()
-            got = g2_in[dx - 1, l].astype(f32)
-            for n in range(3):
-                grad_ref[n, l] += got[:, n * units : (n + 1) * units]
-
     loop(local, collect)
 
     for d in range(1, nf):
         with scope("wait_tg"):
             put(tg_s.at[0], tg_s.at[0], so.at[d], ro.at[d], (k, e, f_at(d))).wait()
     pltpu.make_async_copy(tg_s.at[0], tg_s.at[0], own_sems.at[3]).wait()
+    copies[1].wait()
+    copies[2].wait()
 
     for de in range(ne):
         for d in range(nf):
@@ -624,15 +651,16 @@
 
     sizes = (nk, ne, nf, local, cap, token_count, rows, units)
 
+    held = []
+
     def vm(*shape, kind=bf):
+        held.append(math.prod(shape) * jnp.dtype(kind).itemsize)
         return pltpu.VMEM(shape, kind)
 
     def sem(*shape):
         return pltpu.SemaphoreType.DMA(shape)
 
     scratch = [
-        vm(token_count, width),
-        vm(token_count, width),
         vm(nf, ne, 8, token_count, kind=f32),
         vm(local, depth, 3 * units),
         vm(nf, ne * token_count, depth),
@@ -669,22 +697,27 @@
         sem(chips, local), sem(chips, local),
         sem(4),
     ]
+    grant = sum(held) + MARGIN
+    if 3 * grant > 2 * VMEM_ALL:
+        grant = VMEM_ALL
+    state = jax.ShapeDtypeStruct((3, local, rows, units), f32)
     vmem = pl.BlockSpec(memory_space=pltpu.VMEM)
-    hbm = pl.BlockSpec(memory_space=pl.ANY)
-    token_grad, gates, gradient = pl.pallas_call(
+    hbm = pl.BlockSpec(memory_space=pltpu.HBM)
+    anywhere = pl.BlockSpec(memory_space=pl.ANY)
+    token_grad, gates, gradient, params, moment_first, moment_second = pl.pallas_call(
         functools.partial(kernel, sizes),
         out_shape=(
             jax.ShapeDtypeStruct((token_count, width), bf),
             jax.ShapeDtypeStruct((2, token_count), bf),
-            jax.ShapeDtypeStruct((3, local, rows, units), f32),
+            state, state, state, state,
         ),
-        in_specs=[vmem, vmem, hbm, hbm, hbm],
-        out_specs=(hbm, vmem, vmem),
+        in_specs=[vmem, vmem, vmem, vmem, hbm, hbm, hbm],
+        out_specs=(anywhere, vmem, vmem, vmem, vmem, vmem),
         scratch_shapes=scratch,
         compiler_params=pltpu.CompilerParams(
-            collective_id=0, has_side_effects=True, vmem_limit_bytes=67043328
+            collective_id=0, has_side_effects=True, vmem_limit_bytes=grant
         ),
-    )(expert_ids.T, gate_probs.T, tokens, out_grad, params)
+    )(expert_ids.T, gate_probs.T, tokens, out_grad, params, moment_first, moment_second)
     new_params, new_first, new_second = adam_update(params, gradient, moment_first, moment_second)
     return (token_grad, gates.T, new_params, new_first, new_second)
 

time: 168 us -> 158 us (0.940)
  Pallas kernels: 158 us -> 147 us
  local copies, waits for them, and re-layouts: 1.49 us -> 5.25 us
  other arithmetic: 8 us -> 4.85 us
    pallas_call x1, Pallas kernels: 158 us -> 147 us  [per_device(): pl.pallas_call(functools.partial(kernel, sizes), out_shape=(jax.ShapeDtyp...]
    unnamed x6 -> x10, local copies, waits for them, and re-layouts: 1.49 us -> 5.25 us
    sub x1, other arithmetic: 8 us -> 4.85 us  [adam_update(): new_params = params - learn_rate * (stepped + weight_decay * params)]
where the time goes in v4:
time: 158 us
  Pallas kernels  147 us (93%)
  local copies, waits for them, and re-layouts  5.25 us (3%)
  other arithmetic  4.85 us (3%)
    pallas_call x1, Pallas kernels, per_device(): pl.pallas_call(functools.partial(kernel, sizes), out_shape=(jax.ShapeDtyp...  147 us
    unnamed x10, local copies, waits for them, and re-layouts  5.25 us
    sub x1, other arithmetic, adam_update(): new_params = params - learn_rate * (stepped + weight_decay * params)  4.85 us

profile of v4, /device:TPU:0, one launch (start us, length us, event | category | flops | bytes accessed | tf_op | source)
XLA Modules:
  0.0 157.7 jit_solution(17395306262037281156)
XLA Ops:
  0.6 0.0 copy-start
  0.6 1.2 copy-done
  1.9 0.0 copy-start.1
  1.9 1.2 copy-done.1
  3.1 0.0 copy-start.2
  3.1 0.7 copy-done.2
  3.8 0.0 copy-start.3
  3.8 0.7 copy-done.3
  4.4 147.0 %shard_map.110 = (bf16[128,4096]{1,0:T(8,128)(2,1)S(1)}, bf16[2,128]{1,0:T(2,128)(2,1)S(1)}, f32[3,4,256,256]{3,2,1,0:T(8,128)S(1)}, f32[3,4,256,256]{3,2,1,0:T(...) custom-call(s32[2,128]{1,0:T(2,128)S(1)} %bitcast.3, bf16[2,128]{1,0:T(2,128)(2,1)S(1)} %bitcast.4, ...), custom_call_target="tpu_custom_call" | custom-call | tf_op jit(solution)/shard_map/pallas_call | solution.py:707
  151.4 4.9 %multiply_subtract_fusion = (f32[3,4,256,256]{3,2,1,0:T(8,128)}, f32[3,4,256,256]{3,2,1,0:T(8,128)}, f32[3,4,256,256]{3,2,1,0:T(8,128)}) fusion(f32[3,4,256,256]{3,2,1,0:T(8,128)S(1)} %get-tuple-element.13, f32[3,4,256,256]{3,2,1,0:T(8,128)S(1)} %get-tuple-element.15, f32[3,4,256,256]{3,2,1,0:T(8,128)S(1)} %get-tuple-element.14, ...), kind=kLoop, calls=%fused_computation.2 | loop fusion | flops 11796480 | bytes 22020096 | tf_op jit(solution)/shard_map/sub | solution.py:29
  156.3 1.0 copy.14
  157.2 0.5 copy.15
Async XLA Ops:
  0.6 1.2 copy-start
  1.9 1.2 copy-start.1
  3.1 0.7 copy-start.2
  3.8 0.7 copy-start.3

commit v5 on v4

--- a/solution.py
+++ b/solution.py
@@ -132,8 +132,19 @@
 
     at_edge = (f == 0) | (f == nf - 1)
 
-    def far(n):
-        return jnp.where(at_edge, nf + 1 - n, n) if n > 1 else 1
+    def arrivals(a, place):
+        if place == 0:
+            return [1, *range(nf - 1, 1, -1)]
+        ends = [nf - 1, 0] if a == 0 else [0, nf - 1]
+        inner = sorted(set(range(1, nf - 1)) - {place}, key=lambda g: abs(g - place))
+        return ends + inner
+
+    def arriving(a, n):
+        place = jnp.where(f < nf // 2, f, nf - 1 - f)
+        g = jnp.int32(arrivals(a, 0)[n])
+        for p in range(1, nf // 2):
+            g = jnp.where(place == p, arrivals(a, p)[n], g)
+        return jnp.where(f < nf // 2, g, nf - 1 - g)
 
     arrays = ((tok_ref, tokb), (og_ref, ogb))
     wide = (pl.ds(0, 2 * units), pl.ds(2 * units, units))
@@ -189,16 +200,25 @@
         for d in range(nf):
             if de or d:
                 info_copy(de, d).start()
-    for t in range(1, nf):
-        sides(far(t), functools.partial(z_start, 0))
+    def z_starts(a, distances):
+        for t in distances:
+            sides(t, functools.partial(z_start, a))
+
+    @pl.when(at_edge)
+    def _():
+        z_starts(0, range(nf - 1, 0, -1))
+        z_starts(1, [1])
+
+    @pl.when(jnp.logical_not(at_edge))
+    def _():
+        z_starts(0, range(1, nf))
+        z_starts(1, range(1, nf))
+
     y_own_start(0)
     for a in range(2):
         for dx in range(1, chips):
             w_chip(a, dx, k).start()
         w_core(a, 0, k).start()
-        if a == 0:
-            for t in range(1, nf):
-                sides(far(t), functools.partial(z_start, 1))
 
     copies[1].start()
     copies[2].start()
@@ -206,10 +226,16 @@
         for kk in range(nk):
             dst[f, mine(e), cut(kk)] = src[:, strip(kk, f)]
 
-    for t in range(1, nf):
-        sides(far(t), functools.partial(z_pass, 0))
-        if t == 1:
+    for n in range(nf - 1):
+        z_pass(0, arriving(0, n))
+        if n == 0:
             y_own_start(1)
+
+    @pl.when(at_edge)
+    def _():
+        z_starts(1, range(nf - 1, 1, -1))
+
+    z_pass(1, arriving(1, 0))
     for de in range(ne):
         for d in range(nf):
             if de or d:
@@ -299,11 +325,10 @@
 
     near = jnp.where(f < nf // 2, 1, -1)
 
-    def rs_chain(a, first=0):
+    def rs_chain(a, sign, first=0):
         def steps(n):
             t = n + first
-            for sign in (near, -near):
-                rs_step(a, jnp.where(sign > 0, nf - 1 - t, t), sign)
+            rs_step(a, jnp.where(sign > 0, nf - 1 - t, t), sign)
 
         loop(nf - 1 - first, steps)
 
@@ -320,18 +345,17 @@
     w_pass(0)
     w_done(0)
     partial_sum(0, f)
-    for t in range(1, nf):
-        both(far(t), functools.partial(partial_sum, 0))
-        if t == min(2, nf - 1):
-            sides(1, functools.partial(z_pass, 1))
+    for n in range(nf - 1):
+        partial_sum(0, arriving(0, n))
 
     @pl.when(at_edge)
     def _():
-        rs_chain(0)
-
-    w_pass(1)
-    for t in range(2, nf):
-        sides(far(t), functools.partial(z_pass, 1))
+        rs_chain(0, near)
+
+    for n in range(1, nf - 1):
+        z_pass(1, arriving(1, n))
+        if n == 1:
+            w_pass(1)
     w_done(1)
 
     @pl.when(jnp.logical_not(at_edge))
@@ -339,19 +363,16 @@
         rs_step(0, jnp.where(near > 0, nf - 1, 0), near)
 
     partial_sum(1, f)
-    for t in range(1, nf):
-        both(far(t), functools.partial(partial_sum, 1))
-        if t == 1:
-
-            @pl.when(jnp.logical_not(at_edge))
-            def _():
-                rs_step(0, jnp.where(near > 0, 0, nf - 1), -near)
+    for n in range(nf - 1):
+        partial_sum(1, arriving(1, n))
 
     @pl.when(jnp.logical_not(at_edge))
     def _():
-        rs_chain(0, 1)
-
-    rs_chain(1)
+        rs_chain(0, near, 1)
+        rs_chain(0, -near)
+
+    rs_chain(1, near)
+    rs_chain(1, -near)
 
     for a, got in enumerate((pre_r, prj_r)):
         for spot, edge in ((f, 0), (nf, nf - 1)):
@@ -394,6 +415,22 @@
     def has(sign):
         return (f + sign >= 0) & (f + sign < nf)
 
+    def ag_first():
+        held = dl.at[0, group(f), :]
+
+        def direct(g):
+            put(held, held, sa.at[0, g], ra.at[0, f], (k, e, g)).start()
+
+        @pl.when(at_edge)
+        def _():
+            for t in range(nf - 1, 0, -1):
+                sides(t, direct)
+
+        @pl.when(jnp.logical_not(at_edge))
+        def _():
+            for t in range(1, nf):
+                sides(t, direct)
+
     def ag_own(h):
         for sign, spot in ((1, f), (-1, nf)):
 
@@ -409,9 +446,11 @@
             with scope("wait_ag"):
                 ag_copy(h, g, sign, g).wait_recv()
 
-            @pl.when(has(sign))
-            def _():
-                ag_copy(h, g, sign, g).start()
+            if h:
+
+                @pl.when(has(sign))
+                def _():
+                    ag_copy(h, g, sign, g).start()
 
     nothing = jnp.zeros((1, ne * tcount), f32)
     parts = (nothing, nothing)
@@ -419,7 +458,9 @@
     for h in range(local):
         with scope("middle"):
             parts = middle(jnp.int32(h), parts)
-        if h < ahead:
+        if h == 0:
+            ag_first()
+        elif h < ahead:
             ag_own(h)
 
     for ee in range(ne):
@@ -533,7 +574,7 @@
 
     loop(local, own_rows)
     returned(f)
-    tail = min(2, local)
+    tail = 1
     head = local - tail
     for l in range(head):
         for t in range(1, nf):
@@ -541,11 +582,10 @@
                 ag_step(l, t, sign)
             if t == 1 and l + ahead < local:
                 ag_own(l + ahead)
-            if t == 2 and l:
-                to_chip(jnp.int32(l - 1))
         to_core(jnp.int32(l))
         for t in range(1, nf):
             both(t, functools.partial(slot_rows, jnp.int32(l)))
+        to_chip(jnp.int32(l))
         if l == 0:
             final(f)
         else:
@@ -554,8 +594,6 @@
         for l in range(head, local):
             for sign in (1, -1):
                 ag_step(l, t, sign)
-        if t == 1 and head:
-            to_chip(jnp.int32(head - 1))
         if t == nf - 1:
             for l in range(head, local):
                 to_core(jnp.int32(l))
@@ -606,7 +644,13 @@
                 z_whole(a, g).wait_send()
                 rs_copy(a, g, 1).wait_send()
 
-    for h in range(local):
+    for g in range(nf):
+
+        @pl.when(f != g)
+        def _():
+            put(dl.at[0, group(f), :], dl.at[0, group(f), :], sa.at[0, g], ra.at[0, f], (k, e, g)).wait_send()
+
+    for h in range(1, local):
         for g in range(nf):
             sign = jnp.where(f >= g, 1, -1)
 

time: 158 us -> 159 us (level)
  no operation moved by 1% of the time
where the time goes in v5:
time: 159 us
  Pallas kernels  148 us (93%)
  local copies, waits for them, and re-layouts  5.25 us (3%)
  other arithmetic  4.85 us (3%)
    pallas_call x1, Pallas kernels, per_device(): pl.pallas_call(functools.partial(kernel, sizes), out_shape=(jax.ShapeDtyp...  148 us
    unnamed x10, local copies, waits for them, and re-layouts  5.25 us
    sub x1, other arithmetic, adam_update(): new_params = params - learn_rate * (stepped + weight_decay * params)  4.85 us

profile of v5, /device:TPU:0, one launch (start us, length us, event | category | flops | bytes accessed | tf_op | source)
XLA Modules:
  0.0 159.2 jit_solution(10985357081419997060)
XLA Ops:
  0.6 0.0 copy-start
  0.6 1.2 copy-done
  1.9 0.0 copy-start.1
  1.9 1.2 copy-done.1
  3.1 0.0 copy-start.2
  3.1 0.7 copy-done.2
  3.8 0.0 copy-start.3
  3.8 0.7 copy-done.3
  4.4 148.4 %shard_map.110 = (bf16[128,4096]{1,0:T(8,128)(2,1)S(1)}, bf16[2,128]{1,0:T(2,128)(2,1)S(1)}, f32[3,4,256,256]{3,2,1,0:T(8,128)S(1)}, f32[3,4,256,256]{3,2,1,0:T(...) custom-call(s32[2,128]{1,0:T(2,128)S(1)} %bitcast.3, bf16[2,128]{1,0:T(2,128)(2,1)S(1)} %bitcast.4, ...), custom_call_target="tpu_custom_call" | custom-call | tf_op jit(solution)/shard_map/pallas_call | solution.py:751
  152.9 4.9 %multiply_subtract_fusion = (f32[3,4,256,256]{3,2,1,0:T(8,128)}, f32[3,4,256,256]{3,2,1,0:T(8,128)}, f32[3,4,256,256]{3,2,1,0:T(8,128)}) fusion(f32[3,4,256,256]{3,2,1,0:T(8,128)S(1)} %get-tuple-element.13, f32[3,4,256,256]{3,2,1,0:T(8,128)S(1)} %get-tuple-element.15, f32[3,4,256,256]{3,2,1,0:T(8,128)S(1)} %get-tuple-element.14, ...), kind=kLoop, calls=%fused_computation.2 | loop fusion | flops 11796480 | bytes 22020096 | tf_op jit(solution)/shard_map/sub | solution.py:29
  157.7 1.0 copy.14
  158.7 0.5 copy.15
Async XLA Ops:
  0.6 1.2 copy-start
  1.9 1.2 copy-start.1
  3.1 0.7 copy-start.2
  3.8 0.7 copy-start.3

commit v6 on v5

--- a/solution.py
+++ b/solution.py
@@ -44,9 +44,9 @@
 
 def kernel(
     sizes,
-    ids_ref, gates_ref, tok_ref, og_ref, params_hbm, first_hbm, second_hbm,
+    ids_ref, gates_ref, tok_hbm, og_hbm, params_hbm, first_hbm, second_hbm,
     tg_ref, gg_ref, grad_ref, par_ref, first_ref, second_ref,
-    info, weights, tokb, ogb, place, inp, ups, pre_s, prj_s, pre_r, prj_r, own, dl, sg,
+    tok_ref, og_ref, info, weights, tokb, ogb, place, inp, ups, pre_s, prj_s, pre_r, prj_r, own, dl, sg,
     ret_r, tg_s, gg_s, gg_r, g1_out, g1_in, g2_out, g2_in,
     si, ri, sz, rz, sy, ry, sw, rw, sv, rv, sp, rp, sa, ra, st, rt, so, ro, sg_sem, rg_sem, s1, r1, s2, r2,
     own_sems,
@@ -102,9 +102,12 @@
         pl.semaphore_signal(barrier, inc=1, device_id=(chip_at(dx, c), e, f), device_id_type=MESH)
         partners += 1
 
-    staged = ((params_hbm, par_ref), (first_hbm, first_ref), (second_hbm, second_ref))
+    staged = (
+        (params_hbm, par_ref), (first_hbm, first_ref), (second_hbm, second_ref), (tok_hbm, tok_ref), (og_hbm, og_ref)
+    )
     copies = [pltpu.make_async_copy(src, dst, own_sems.at[n]) for n, (src, dst) in enumerate(staged)]
-    copies[0].start()
+    for n in (0, 3, 4):
+        copies[n].start()
 
     def iota(shape, dim):
         return lax.broadcasted_iota(jnp.int32, shape, dim)
@@ -123,6 +126,8 @@
     for l in range(local):
         for n in range(3):
             weights[l, cut(k), n * units : (n + 1) * units] = par_ref[n, l].astype(bf)
+    copies[3].wait()
+    copies[4].wait()
     with scope("barrier"):
         pl.semaphore_wait(barrier, partners)
 
@@ -296,17 +301,24 @@
 
             loop(local, expert)
 
+    first = max(1, local // 2)
+    streams = [(pre_s, pre_r, 0, local), (prj_s, prj_r, 0, first)]
+    if first < local:
+        streams.append((prj_s, prj_r, first, local))
+
     def rs_copy(a, g, sign):
-        sent, got = ((pre_s, pre_r), (prj_s, prj_r))[a]
+        sent, got, low, high = streams[a]
         spot = jnp.where((sign < 0) & (g == f - 1), nf, g)
-        return put(sent.at[g], got.at[spot], sp.at[a, g], rp.at[a, spot], (k, e, f + sign))
+        these = pl.ds(low * span, (high - low) * span)
+        return put(sent.at[g, these], got.at[spot, these], sp.at[a, g], rp.at[a, spot], (k, e, f + sign))
 
     def rs_wait(a, spot):
-        got = (pre_r, prj_r)[a]
-        put(got.at[spot], got.at[spot], sp.at[a, 0], rp.at[a, spot], (k, e, f_at(1))).wait_recv()
+        _, got, low, high = streams[a]
+        these = pl.ds(low * span, (high - low) * span)
+        put(got.at[spot, these], got.at[spot, these], sp.at[a, 0], rp.at[a, spot], (k, e, f_at(1))).wait_recv()
 
     def rs_step(a, g, sign):
-        sent, got = ((pre_s, pre_r), (prj_s, prj_r))[a]
+        sent, got, low, high = streams[a]
         behind = f - sign
 
         @pl.when((g - f) * sign > 0)
@@ -316,12 +328,26 @@
                 with scope("wait_rs"):
                     rs_wait(a, g)
 
-                def add(l):
+                def add(n):
+                    l = n + low
                     sent[g, at(l), :] = (sent[g, at(l), :].astype(f32) + got[g, at(l), :].astype(f32)).astype(bf)
 
-                loop(local, add)
+                loop(high - low, add)
 
             rs_copy(a, g, sign).start()
+
+    def rs_own(a):
+        _, got, low, high = streams[a]
+        for spot, edge in ((f, 0), (nf, nf - 1)):
+
+            @pl.when(f == edge)
+            def _():
+                got[spot, low * span : high * span] = jnp.zeros(((high - low) * span, got.shape[2]), bf)
+
+            @pl.when(f != edge)
+            def _():
+                with scope("wait_own"):
+                    rs_wait(a, spot)
 
     near = jnp.where(f < nf // 2, 1, -1)
 
@@ -370,21 +396,6 @@
     def _():
         rs_chain(0, near, 1)
         rs_chain(0, -near)
-
-    rs_chain(1, near)
-    rs_chain(1, -near)
-
-    for a, got in enumerate((pre_r, prj_r)):
-        for spot, edge in ((f, 0), (nf, nf - 1)):
-
-            @pl.when(f == edge)
-            def _():
-                got[spot] = jnp.zeros(got.shape[1:], bf)
-
-            @pl.when(f != edge)
-            def _():
-                with scope("wait_own"):
-                    rs_wait(a, spot)
 
     def middle(l, carry):
         here = at(l)
@@ -455,13 +466,29 @@
     nothing = jnp.zeros((1, ne * tcount), f32)
     parts = (nothing, nothing)
     ahead = 2
-    for h in range(local):
-        with scope("middle"):
-            parts = middle(jnp.int32(h), parts)
-        if h == 0:
-            ag_first()
-        elif h < ahead:
-            ag_own(h)
+    for a in range(1, len(streams)):
+
+        @pl.when(at_edge)
+        def _():
+            rs_chain(a, near)
+
+    for a in range(1, len(streams)):
+
+        @pl.when(jnp.logical_not(at_edge))
+        def _():
+            rs_chain(a, near)
+            rs_chain(a, -near)
+
+        if a == 1:
+            rs_own(0)
+        rs_own(a)
+        for h in range(*streams[a][2:]):
+            with scope("middle"):
+                parts = middle(jnp.int32(h), parts)
+            if h == 0:
+                ag_first()
+            elif h < ahead:
+                ag_own(h)
 
     for ee in range(ne):
         for j in range(2):
@@ -516,7 +543,7 @@
 
                 @pl.when(d == 0)
                 def _():
-                    pltpu.make_async_copy(tg_s.at[g, :, cut(kk)], there, own_sems.at[3]).start()
+                    pltpu.make_async_copy(tg_s.at[g, :, cut(kk)], there, own_sems.at[5]).start()
 
             loop(nk, column)
 
@@ -574,7 +601,7 @@
 
     loop(local, own_rows)
     returned(f)
-    tail = 1
+    tail = min(2, local)
     head = local - tail
     for l in range(head):
         for t in range(1, nf):
@@ -594,8 +621,7 @@
         for l in range(head, local):
             for sign in (1, -1):
                 ag_step(l, t, sign)
-        if t == nf - 1:
-            for l in range(head, local):
+            if t == nf - 1:
                 to_core(jnp.int32(l))
 
         def rows_back(g):
@@ -604,13 +630,15 @@
             returned(g)
 
         both(t, rows_back)
+        if t == nf - 1:
+            to_chip(jnp.int32(head))
     if not head:
         final(f)
-    for n in range(max(tail, nf - 1)):
-        if n < tail:
-            to_chip(jnp.int32(head + n))
-        if n < nf - 1:
-            both(n + 1, final)
+    both(1, final)
+    for l in range(head + 1, local):
+        to_chip(jnp.int32(l))
+    for t in range(2, nf):
+        both(t, final)
     with scope("keep"):
         for l in range(max(head - 1, 0), local):
             keep(jnp.int32(l))
@@ -628,7 +656,7 @@
     for d in range(1, nf):
         with scope("wait_tg"):
             put(tg_s.at[0], tg_s.at[0], so.at[d], ro.at[d], (k, e, f_at(d))).wait()
-    pltpu.make_async_copy(tg_s.at[0], tg_s.at[0], own_sems.at[3]).wait()
+    pltpu.make_async_copy(tg_s.at[0], tg_s.at[0], own_sems.at[5]).wait()
     copies[1].wait()
     copies[2].wait()
 
@@ -642,6 +670,7 @@
         def _():
             for a in range(2):
                 z_whole(a, g).wait_send()
+            for a in range(len(streams)):
                 rs_copy(a, g, 1).wait_send()
 
     for g in range(nf):
@@ -705,6 +734,8 @@
         return pltpu.SemaphoreType.DMA(shape)
 
     scratch = [
+        vm(token_count, width),
+        vm(token_count, width),
         vm(nf, ne, 8, token_count, kind=f32),
         vm(local, depth, 3 * units),
         vm(nf, ne * token_count, depth),
@@ -732,14 +763,14 @@
         sem(2, nf, ne), sem(2, nf, ne),
         sem(2, chips), sem(2, chips),
         sem(2, chips), sem(2, chips),
-        sem(2, nf), sem(2, nf + 1),
+        sem(3, nf), sem(3, nf + 1),
         sem(local, nf + 1), sem(local, nf),
         sem(nf, ne, nk), sem(nf, ne, nk),
         sem(nf), sem(nf),
         sem(ne), sem(ne),
         sem(chips, local), sem(chips, local),
         sem(chips, local), sem(chips, local),
-        sem(4),
+        sem(6),
     ]
     grant = sum(held) + MARGIN
     if 3 * grant > 2 * VMEM_ALL:
@@ -755,13 +786,18 @@
             jax.ShapeDtypeStruct((2, token_count), bf),
             state, state, state, state,
         ),
-        in_specs=[vmem, vmem, vmem, vmem, hbm, hbm, hbm],
+        in_specs=[vmem, vmem, hbm, hbm, hbm, hbm, hbm],
         out_specs=(anywhere, vmem, vmem, vmem, vmem, vmem),
         scratch_shapes=scratch,
         compiler_params=pltpu.CompilerParams(
             collective_id=0, has_side_effects=True, vmem_limit_bytes=grant
         ),
-    )(expert_ids.T, gate_probs.T, tokens, out_grad, params, moment_first, moment_second)
+    )(
+        expert_ids.T,
+        gate_probs.T,
+        *(pltpu.with_memory_space_constraint(a, pltpu.HBM) for a in (tokens, out_grad, params)),
+        *(pltpu.with_memory_space_constraint(a, pltpu.HBM) for a in (moment_first, moment_second)),
+    )
     new_params, new_first, new_second = adam_update(params, gradient, moment_first, moment_second)
     return (token_grad, gates.T, new_params, new_first, new_second)
 

time: 159 us -> 155 us (0.975)
  local copies, waits for them, and re-layouts: 5.25 us -> 2.81 us
  Pallas kernels: 148 us -> 146 us
    unnamed x10 -> x6, local copies, waits for them, and re-layouts: 5.25 us -> 2.81 us
    pallas_call x1, Pallas kernels: 148 us -> 146 us  [per_device(): pl.pallas_call(functools.partial(kernel, sizes), out_shape=(jax.ShapeDtyp...]
where the time goes in v6:
time: 155 us
  Pallas kernels  146 us (94%)
  other arithmetic  4.85 us (3%)
  local copies, waits for them, and re-layouts  2.81 us (2%)
    pallas_call x1, Pallas kernels, per_device(): pl.pallas_call(functools.partial(kernel, sizes), out_shape=(jax.ShapeDtyp...  146 us
    sub x1, other arithmetic, adam_update(): new_params = params - learn_rate * (stepped + weight_decay * params)  4.85 us

profile of v6, /device:TPU:0, one launch (start us, length us, event | category | flops | bytes accessed | tf_op | source)
XLA Modules:
  0.0 154.7 jit_solution(11541445090665418878)
XLA Ops:
  0.6 0.0 copy-start
  0.6 0.7 copy-done
  1.3 0.0 copy-start.1
  1.3 0.7 copy-done.1
  2.0 146.4 %shard_map.110 = (bf16[128,4096]{1,0:T(8,128)(2,1)S(1)}, bf16[2,128]{1,0:T(2,128)(2,1)S(1)}, f32[3,4,256,256]{3,2,1,0:T(8,128)S(1)}, f32[3,4,256,256]{3,2,1,0:T(...) custom-call(s32[2,128]{1,0:T(2,128)S(1)} %bitcast.3, bf16[2,128]{1,0:T(2,128)(2,1)S(1)} %bitcast.4, ...), custom_call_target="tpu_custom_call" | custom-call | tf_op jit(solution)/shard_map/pallas_call | solution.py:782
  148.4 4.9 %multiply_subtract_fusion = (f32[3,4,256,256]{3,2,1,0:T(8,128)}, f32[3,4,256,256]{3,2,1,0:T(8,128)}, f32[3,4,256,256]{3,2,1,0:T(8,128)}) fusion(f32[3,4,256,256]{3,2,1,0:T(8,128)S(1)} %get-tuple-element.13, f32[3,4,256,256]{3,2,1,0:T(8,128)S(1)} %get-tuple-element.15, f32[3,4,256,256]{3,2,1,0:T(8,128)S(1)} %get-tuple-element.14, ...), kind=kLoop, calls=%fused_computation.2 | loop fusion | flops 11796480 | bytes 22020096 | tf_op jit(solution)/shard_map/sub | solution.py:29
  153.3 1.0 copy.14
  154.2 0.5 copy.15
Async XLA Ops:
  0.6 0.7 copy-start
  1.3 0.7 copy-start.1

commit v7 on v5

--- a/solution.py
+++ b/solution.py
@@ -44,9 +44,9 @@
 
 def kernel(
     sizes,
-    ids_ref, gates_ref, tok_ref, og_ref, params_hbm, first_hbm, second_hbm,
+    ids_ref, gates_ref, tok_hbm, og_hbm, params_hbm, first_hbm, second_hbm,
     tg_ref, gg_ref, grad_ref, par_ref, first_ref, second_ref,
-    info, weights, tokb, ogb, place, inp, ups, pre_s, prj_s, pre_r, prj_r, own, dl, sg,
+    tok_ref, og_ref, info, weights, tokb, ogb, place, inp, ups, pre_s, prj_s, pre_r, prj_r, own, dl, sg,
     ret_r, tg_s, gg_s, gg_r, g1_out, g1_in, g2_out, g2_in,
     si, ri, sz, rz, sy, ry, sw, rw, sv, rv, sp, rp, sa, ra, st, rt, so, ro, sg_sem, rg_sem, s1, r1, s2, r2,
     own_sems,
@@ -102,9 +102,12 @@
         pl.semaphore_signal(barrier, inc=1, device_id=(chip_at(dx, c), e, f), device_id_type=MESH)
         partners += 1
 
-    staged = ((params_hbm, par_ref), (first_hbm, first_ref), (second_hbm, second_ref))
+    staged = (
+        (params_hbm, par_ref), (first_hbm, first_ref), (second_hbm, second_ref), (tok_hbm, tok_ref), (og_hbm, og_ref)
+    )
     copies = [pltpu.make_async_copy(src, dst, own_sems.at[n]) for n, (src, dst) in enumerate(staged)]
-    copies[0].start()
+    for n in (0, 3, 4):
+        copies[n].start()
 
     def iota(shape, dim):
         return lax.broadcasted_iota(jnp.int32, shape, dim)
@@ -123,6 +126,8 @@
     for l in range(local):
         for n in range(3):
             weights[l, cut(k), n * units : (n + 1) * units] = par_ref[n, l].astype(bf)
+    copies[3].wait()
+    copies[4].wait()
     with scope("barrier"):
         pl.semaphore_wait(barrier, partners)
 
@@ -296,17 +301,14 @@
 
             loop(local, expert)
 
-    def rs_copy(a, g, sign):
-        sent, got = ((pre_s, pre_r), (prj_s, prj_r))[a]
+    def rs_copy(g, sign):
         spot = jnp.where((sign < 0) & (g == f - 1), nf, g)
-        return put(sent.at[g], got.at[spot], sp.at[a, g], rp.at[a, spot], (k, e, f + sign))
-
-    def rs_wait(a, spot):
-        got = (pre_r, prj_r)[a]
-        put(got.at[spot], got.at[spot], sp.at[a, 0], rp.at[a, spot], (k, e, f_at(1))).wait_recv()
-
-    def rs_step(a, g, sign):
-        sent, got = ((pre_s, pre_r), (prj_s, prj_r))[a]
+        return put(pre_s.at[g], pre_r.at[spot], sp.at[0, g], rp.at[0, spot], (k, e, f + sign))
+
+    def rs_wait(spot):
+        put(pre_r.at[spot], pre_r.at[spot], sp.at[0, 0], rp.at[0, spot], (k, e, f_at(1))).wait_recv()
+
+    def rs_step(g, sign):
         behind = f - sign
 
         @pl.when((g - f) * sign > 0)
@@ -314,27 +316,34 @@
             @pl.when((behind >= 0) & (behind < nf))
             def _():
                 with scope("wait_rs"):
-                    rs_wait(a, g)
+                    rs_wait(g)
 
                 def add(l):
-                    sent[g, at(l), :] = (sent[g, at(l), :].astype(f32) + got[g, at(l), :].astype(f32)).astype(bf)
+                    pre_s[g, at(l), :] = (pre_s[g, at(l), :].astype(f32) + pre_r[g, at(l), :].astype(f32)).astype(bf)
 
                 loop(local, add)
 
-            rs_copy(a, g, sign).start()
+            rs_copy(g, sign).start()
+
+    def prj_copy(g):
+        return put(prj_s.at[g], prj_r.at[f], sp.at[1, g], rp.at[1, f], (k, e, g))
+
+    def prj_wait(g):
+        with scope("wait_prj"):
+            put(prj_r.at[g], prj_r.at[g], sp.at[1, g], rp.at[1, g], (k, e, g)).wait_recv()
 
     near = jnp.where(f < nf // 2, 1, -1)
 
-    def rs_chain(a, sign, first=0):
+    def rs_chain(sign, first=0):
         def steps(n):
             t = n + first
-            rs_step(a, jnp.where(sign > 0, nf - 1 - t, t), sign)
+            rs_step(jnp.where(sign > 0, nf - 1 - t, t), sign)
 
         loop(nf - 1 - first, steps)
 
     def both(t, work):
         def side(n):
-            g = f + (1 - 2 * n) * t
+            g = f + near * (1 - 2 * n) * t
 
             @pl.when((g >= 0) & (g < nf))
             def _():
@@ -350,7 +359,7 @@
 
     @pl.when(at_edge)
     def _():
-        rs_chain(0, near)
+        rs_chain(near)
 
     for n in range(1, nf - 1):
         z_pass(1, arriving(1, n))
@@ -360,37 +369,48 @@
 
     @pl.when(jnp.logical_not(at_edge))
     def _():
-        rs_step(0, jnp.where(near > 0, nf - 1, 0), near)
+        rs_step(jnp.where(near > 0, nf - 1, 0), near)
 
     partial_sum(1, f)
     for n in range(nf - 1):
         partial_sum(1, arriving(1, n))
 
+    def prj_start(g):
+        prj_copy(g).start()
+
+    @pl.when(at_edge)
+    def _():
+        for t in range(nf - 1, 0, -1):
+            sides(t, prj_start)
+
     @pl.when(jnp.logical_not(at_edge))
     def _():
-        rs_chain(0, near, 1)
-        rs_chain(0, -near)
-
-    rs_chain(1, near)
-    rs_chain(1, -near)
-
-    for a, got in enumerate((pre_r, prj_r)):
-        for spot, edge in ((f, 0), (nf, nf - 1)):
-
-            @pl.when(f == edge)
-            def _():
-                got[spot] = jnp.zeros(got.shape[1:], bf)
-
-            @pl.when(f != edge)
-            def _():
-                with scope("wait_own"):
-                    rs_wait(a, spot)
+        rs_chain(near, 1)
+        for t in range(1, nf):
+            sides(t, prj_start)
+        rs_chain(-near)
+
+    for spot, edge in ((f, 0), (nf, nf - 1)):
+
+        @pl.when(f == edge)
+        def _():
+            pre_r[spot] = jnp.zeros(pre_r.shape[1:], bf)
+
+        @pl.when(f != edge)
+        def _():
+            with scope("wait_own"):
+                rs_wait(spot)
+
+    for d in range(1, nf):
+        prj_wait(f_at(d))
 
     def middle(l, carry):
         here = at(l)
         gate = own[here, :units] + pre_r[f, here, :units].astype(f32) + pre_r[nf, here, :units].astype(f32)
         up = own[here, units : 2 * units] + pre_r[f, here, units:].astype(f32) + pre_r[nf, here, units:].astype(f32)
-        proj = own[here, 2 * units :] + prj_r[f, here, :].astype(f32) + prj_r[nf, here, :].astype(f32)
+        proj = own[here, 2 * units :]
+        for d in range(1, nf):
+            proj += prj_r[f_at(d), here, :].astype(f32)
         zero, one = choose(f, (l * span).astype(f32), span)
         scale = jnp.sum(
             jnp.where(zero, codes(f, 2), 0.0) + jnp.where(one, codes(f, 3), 0.0), axis=1, keepdims=True
@@ -516,7 +536,7 @@
 
                 @pl.when(d == 0)
                 def _():
-                    pltpu.make_async_copy(tg_s.at[g, :, cut(kk)], there, own_sems.at[3]).start()
+                    pltpu.make_async_copy(tg_s.at[g, :, cut(kk)], there, own_sems.at[5]).start()
 
             loop(nk, column)
 
@@ -574,7 +594,7 @@
 
     loop(local, own_rows)
     returned(f)
-    tail = 1
+    tail = min(2, local)
     head = local - tail
     for l in range(head):
         for t in range(1, nf):
@@ -594,8 +614,7 @@
         for l in range(head, local):
             for sign in (1, -1):
                 ag_step(l, t, sign)
-        if t == nf - 1:
-            for l in range(head, local):
+            if t == nf - 1:
                 to_core(jnp.int32(l))
 
         def rows_back(g):
@@ -603,14 +622,24 @@
                 slot_rows(jnp.int32(l), g)
             returned(g)
 
+        if t == nf - 1:
+            to_chip(jnp.int32(head))
         both(t, rows_back)
     if not head:
         final(f)
-    for n in range(max(tail, nf - 1)):
-        if n < tail:
-            to_chip(jnp.int32(head + n))
-        if n < nf - 1:
-            both(n + 1, final)
+    for l in range(head + 1, local):
+        to_chip(jnp.int32(l))
+
+    @pl.when(at_edge)
+    def _():
+        for t in [*range(2, nf - 1), 1, nf - 1]:
+            both(t, final)
+
+    @pl.when(jnp.logical_not(at_edge))
+    def _():
+        for t in range(1, nf):
+            both(t, final)
+
     with scope("keep"):
         for l in range(max(head - 1, 0), local):
             keep(jnp.int32(l))
@@ -628,7 +657,7 @@
     for d in range(1, nf):
         with scope("wait_tg"):
             put(tg_s.at[0], tg_s.at[0], so.at[d], ro.at[d], (k, e, f_at(d))).wait()
-    pltpu.make_async_copy(tg_s.at[0], tg_s.at[0], own_sems.at[3]).wait()
+    pltpu.make_async_copy(tg_s.at[0], tg_s.at[0], own_sems.at[5]).wait()
     copies[1].wait()
     copies[2].wait()
 
@@ -642,7 +671,8 @@
         def _():
             for a in range(2):
                 z_whole(a, g).wait_send()
-                rs_copy(a, g, 1).wait_send()
+            rs_copy(g, 1).wait_send()
+            prj_copy(g).wait_send()
 
     for g in range(nf):
 
@@ -705,6 +735,8 @@
         return pltpu.SemaphoreType.DMA(shape)
 
     scratch = [
+        vm(token_count, width),
+        vm(token_count, width),
         vm(nf, ne, 8, token_count, kind=f32),
         vm(local, depth, 3 * units),
         vm(nf, ne * token_count, depth),
@@ -715,7 +747,7 @@
         vm(nf, slots, 2 * units),
         vm(nf, slots, units),
         vm(nf + 1, slots, 2 * units),
-        vm(nf + 1, slots, units),
+        vm(nf, slots, units),
         vm(slots, 3 * units, kind=f32),
         vm(local, nf * span, 3 * units),
         vm(nf, slots, depth),
@@ -739,7 +771,7 @@
         sem(ne), sem(ne),
         sem(chips, local), sem(chips, local),
         sem(chips, local), sem(chips, local),
-        sem(4),
+        sem(6),
     ]
     grant = sum(held) + MARGIN
     if 3 * grant > 2 * VMEM_ALL:
@@ -755,13 +787,18 @@
             jax.ShapeDtypeStruct((2, token_count), bf),
             state, state, state, state,
         ),
-        in_specs=[vmem, vmem, vmem, vmem, hbm, hbm, hbm],
+        in_specs=[vmem, vmem, hbm, hbm, hbm, hbm, hbm],
         out_specs=(anywhere, vmem, vmem, vmem, vmem, vmem),
         scratch_shapes=scratch,
         compiler_params=pltpu.CompilerParams(
             collective_id=0, has_side_effects=True, vmem_limit_bytes=grant
         ),
-    )(expert_ids.T, gate_probs.T, tokens, out_grad, params, moment_first, moment_second)
+    )(
+        expert_ids.T,
+        gate_probs.T,
+        *(pltpu.with_memory_space_constraint(a, pltpu.HBM) for a in (tokens, out_grad, params)),
+        *(pltpu.with_memory_space_constraint(a, pltpu.HBM) for a in (moment_first, moment_second)),
+    )
     new_params, new_first, new_second = adam_update(params, gradient, moment_first, moment_second)
     return (token_grad, gates.T, new_params, new_first, new_second)
 

time: 159 us -> 155 us (0.975)
  local copies, waits for them, and re-layouts: 5.25 us -> 2.81 us
  Pallas kernels: 148 us -> 146 us
    unnamed x10 -> x6, local copies, waits for them, and re-layouts: 5.25 us -> 2.81 us
    pallas_call x1, Pallas kernels: 148 us -> 146 us  [per_device(): pl.pallas_call(functools.partial(kernel, sizes), out_shape=(jax.ShapeDtyp...]
where the time goes in v7:
time: 155 us
  Pallas kernels  146 us (94%)
  other arithmetic  4.85 us (3%)
  local copies, waits for them, and re-layouts  2.81 us (2%)
    pallas_call x1, Pallas kernels, per_device(): pl.pallas_call(functools.partial(kernel, sizes), out_shape=(jax.ShapeDtyp...  146 us
    sub x1, other arithmetic, adam_update(): new_params = params - learn_rate * (stepped + weight_decay * params)  4.85 us

profile of v7, /device:TPU:0, one launch (start us, length us, event | category | flops | bytes accessed | tf_op | source)
XLA Modules:
  0.0 154.6 jit_solution(3891777413166044521)
XLA Ops:
  0.6 0.0 copy-start
  0.6 0.7 copy-done
  1.3 0.0 copy-start.1
  1.3 0.7 copy-done.1
  2.0 146.3 %shard_map.110 = (bf16[128,4096]{1,0:T(8,128)(2,1)S(1)}, bf16[2,128]{1,0:T(2,128)(2,1)S(1)}, f32[3,4,256,256]{3,2,1,0:T(8,128)S(1)}, f32[3,4,256,256]{3,2,1,0:T(...) custom-call(s32[2,128]{1,0:T(2,128)S(1)} %bitcast.3, bf16[2,128]{1,0:T(2,128)(2,1)S(1)} %bitcast.4, ...), custom_call_target="tpu_custom_call" | custom-call | tf_op jit(solution)/shard_map/pallas_call | solution.py:783
  148.2 4.9 %multiply_subtract_fusion = (f32[3,4,256,256]{3,2,1,0:T(8,128)}, f32[3,4,256,256]{3,2,1,0:T(8,128)}, f32[3,4,256,256]{3,2,1,0:T(8,128)}) fusion(f32[3,4,256,256]{3,2,1,0:T(8,128)S(1)} %get-tuple-element.13, f32[3,4,256,256]{3,2,1,0:T(8,128)S(1)} %get-tuple-element.15, f32[3,4,256,256]{3,2,1,0:T(8,128)S(1)} %get-tuple-element.14, ...), kind=kLoop, calls=%fused_computation.2 | loop fusion | flops 11796480 | bytes 22020096 | tf_op jit(solution)/shard_map/sub | solution.py:29
  153.1 1.0 copy.14
  154.1 0.5 copy.15
Async XLA Ops:
  0.6 0.7 copy-start
  1.3 0.7 copy-start.1

commit v8 on v7

--- a/solution.py
+++ b/solution.py
@@ -139,7 +139,7 @@
 
     def arrivals(a, place):
         if place == 0:
-            return [1, *range(nf - 1, 1, -1)]
+            return [nf - 1, 1, *range(nf - 2, 1, -1)] if a == 0 else [1, *range(nf - 1, 1, -1)]
         ends = [nf - 1, 0] if a == 0 else [0, nf - 1]
         inner = sorted(set(range(1, nf - 1)) - {place}, key=lambda g: abs(g - place))
         return ends + inner
@@ -220,6 +220,7 @@
         z_starts(1, range(1, nf))
 
     y_own_start(0)
+    y_own_start(1)
     for a in range(2):
         for dx in range(1, chips):
             w_chip(a, dx, k).start()
@@ -233,8 +234,6 @@
 
     for n in range(nf - 1):
         z_pass(0, arriving(0, n))
-        if n == 0:
-            y_own_start(1)
 
     @pl.when(at_edge)
     def _():
@@ -372,11 +371,18 @@
         rs_step(jnp.where(near > 0, nf - 1, 0), near)
 
     partial_sum(1, f)
+    def prj_start(g):
+        prj_copy(g).start()
+
     for n in range(nf - 1):
         partial_sum(1, arriving(1, n))
 
-    def prj_start(g):
-        prj_copy(g).start()
+        @pl.when(jnp.logical_not(at_edge))
+        def _():
+            prj_start(arriving(1, n))
+            if n == 1:
+                rs_chain(near, 1)
+
 
     @pl.when(at_edge)
     def _():
@@ -385,9 +391,6 @@
 
     @pl.when(jnp.logical_not(at_edge))
     def _():
-        rs_chain(near, 1)
-        for t in range(1, nf):
-            sides(t, prj_start)
         rs_chain(-near)
 
     for spot, edge in ((f, 0), (nf, nf - 1)):
@@ -625,6 +628,12 @@
         if t == nf - 1:
             to_chip(jnp.int32(head))
         both(t, rows_back)
+        if t == 2 and head:
+
+            @pl.when(jnp.logical_not(at_edge))
+            def _():
+                final(f + near)
+
     if not head:
         final(f)
     for l in range(head + 1, local):
@@ -637,7 +646,10 @@
 
     @pl.when(jnp.logical_not(at_edge))
     def _():
-        for t in range(1, nf):
+        if not head:
+            final(f + near)
+        final(f - near)
+        for t in range(2, nf):
             both(t, final)
 
     with scope("keep"):

time: 155 us -> 152 us (0.981)
  Pallas kernels: 146 us -> 144 us
    pallas_call x1, Pallas kernels: 146 us -> 144 us  [per_device(): pl.pallas_call(functools.partial(kernel, sizes), out_shape=(jax.ShapeDtyp...]
where the time goes in v8:
time: 152 us
  Pallas kernels  144 us (95%)
  other arithmetic  4.85 us (3%)
  local copies, waits for them, and re-layouts  2.81 us (2%)
    pallas_call x1, Pallas kernels, per_device(): pl.pallas_call(functools.partial(kernel, sizes), out_shape=(jax.ShapeDtyp...  144 us
    sub x1, other arithmetic, adam_update(): new_params = params - learn_rate * (stepped + weight_decay * params)  4.85 us

profile of v8, /device:TPU:0, one launch (start us, length us, event | category | flops | bytes accessed | tf_op | source)
XLA Modules:
  0.0 152.0 jit_solution(16788895518590689582)
XLA Ops:
  0.6 0.0 copy-start
  0.6 0.7 copy-done
  1.3 0.0 copy-start.1
  1.3 0.7 copy-done.1
  2.0 143.7 %shard_map.110 = (bf16[128,4096]{1,0:T(8,128)(2,1)S(1)}, bf16[2,128]{1,0:T(2,128)(2,1)S(1)}, f32[3,4,256,256]{3,2,1,0:T(8,128)S(1)}, f32[3,4,256,256]{3,2,1,0:T(...) custom-call(s32[2,128]{1,0:T(2,128)S(1)} %bitcast.3, bf16[2,128]{1,0:T(2,128)(2,1)S(1)} %bitcast.4, ...), custom_call_target="tpu_custom_call" | custom-call | tf_op jit(solution)/shard_map/pallas_call | solution.py:795
  145.7 4.9 %multiply_subtract_fusion = (f32[3,4,256,256]{3,2,1,0:T(8,128)}, f32[3,4,256,256]{3,2,1,0:T(8,128)}, f32[3,4,256,256]{3,2,1,0:T(8,128)}) fusion(f32[3,4,256,256]{3,2,1,0:T(8,128)S(1)} %get-tuple-element.13, f32[3,4,256,256]{3,2,1,0:T(8,128)S(1)} %get-tuple-element.15, f32[3,4,256,256]{3,2,1,0:T(8,128)S(1)} %get-tuple-element.14, ...), kind=kLoop, calls=%fused_computation.2 | loop fusion | flops 11796480 | bytes 22020096 | tf_op jit(solution)/shard_map/sub | solution.py:29
  150.6 1.0 copy.14
  151.5 0.5 copy.15
Async XLA Ops:
  0.6 0.7 copy-start
  1.3 0.7 copy-start.1

commit v9 on v8

--- a/solution.py
+++ b/solution.py
@@ -300,14 +300,19 @@
 
             loop(local, expert)
 
-    def rs_copy(g, sign):
+    streams = ((pre_s, pre_r), (prj_s, prj_r))
+
+    def rs_copy(a, g, sign):
+        sent, got = streams[a]
         spot = jnp.where((sign < 0) & (g == f - 1), nf, g)
-        return put(pre_s.at[g], pre_r.at[spot], sp.at[0, g], rp.at[0, spot], (k, e, f + sign))
-
-    def rs_wait(spot):
-        put(pre_r.at[spot], pre_r.at[spot], sp.at[0, 0], rp.at[0, spot], (k, e, f_at(1))).wait_recv()
-
-    def rs_step(g, sign):
+        return put(sent.at[g], got.at[spot], sp.at[a, g], rp.at[a, spot], (k, e, f + sign))
+
+    def rs_wait(a, spot):
+        got = streams[a][1]
+        put(got.at[spot], got.at[spot], sp.at[a, 0], rp.at[a, spot], (k, e, f_at(1))).wait_recv()
+
+    def rs_step(a, g, sign):
+        sent, got = streams[a]
         behind = f - sign
 
         @pl.when((g - f) * sign > 0)
@@ -315,28 +320,21 @@
             @pl.when((behind >= 0) & (behind < nf))
             def _():
                 with scope("wait_rs"):
-                    rs_wait(g)
+                    rs_wait(a, g)
 
                 def add(l):
-                    pre_s[g, at(l), :] = (pre_s[g, at(l), :].astype(f32) + pre_r[g, at(l), :].astype(f32)).astype(bf)
+                    sent[g, at(l), :] = (sent[g, at(l), :].astype(f32) + got[g, at(l), :].astype(f32)).astype(bf)
 
                 loop(local, add)
 
-            rs_copy(g, sign).start()
-
-    def prj_copy(g):
-        return put(prj_s.at[g], prj_r.at[f], sp.at[1, g], rp.at[1, f], (k, e, g))
-
-    def prj_wait(g):
-        with scope("wait_prj"):
-            put(prj_r.at[g], prj_r.at[g], sp.at[1, g], rp.at[1, g], (k, e, g)).wait_recv()
+            rs_copy(a, g, sign).start()
 
     near = jnp.where(f < nf // 2, 1, -1)
 
-    def rs_chain(sign, first=0):
+    def rs_chain(a, sign, first=0):
         def steps(n):
             t = n + first
-            rs_step(jnp.where(sign > 0, nf - 1 - t, t), sign)
+            rs_step(a, jnp.where(sign > 0, nf - 1 - t, t), sign)
 
         loop(nf - 1 - first, steps)
 
@@ -358,7 +356,7 @@
 
     @pl.when(at_edge)
     def _():
-        rs_chain(near)
+        rs_chain(0, near)
 
     for n in range(1, nf - 1):
         z_pass(1, arriving(1, n))
@@ -368,52 +366,41 @@
 
     @pl.when(jnp.logical_not(at_edge))
     def _():
-        rs_step(jnp.where(near > 0, nf - 1, 0), near)
+        rs_step(0, jnp.where(near > 0, nf - 1, 0), near)
 
     partial_sum(1, f)
-    def prj_start(g):
-        prj_copy(g).start()
-
     for n in range(nf - 1):
         partial_sum(1, arriving(1, n))
-
-        @pl.when(jnp.logical_not(at_edge))
-        def _():
-            prj_start(arriving(1, n))
-            if n == 1:
-                rs_chain(near, 1)
-
-
-    @pl.when(at_edge)
-    def _():
-        for t in range(nf - 1, 0, -1):
-            sides(t, prj_start)
+        if n == 1:
+
+            @pl.when(jnp.logical_not(at_edge))
+            def _():
+                rs_chain(0, near, 1)
 
     @pl.when(jnp.logical_not(at_edge))
     def _():
-        rs_chain(-near)
-
-    for spot, edge in ((f, 0), (nf, nf - 1)):
-
-        @pl.when(f == edge)
-        def _():
-            pre_r[spot] = jnp.zeros(pre_r.shape[1:], bf)
-
-        @pl.when(f != edge)
-        def _():
-            with scope("wait_own"):
-                rs_wait(spot)
-
-    for d in range(1, nf):
-        prj_wait(f_at(d))
+        rs_chain(0, -near)
+
+    rs_chain(1, near)
+    rs_chain(1, -near)
+
+    for a, (_, got) in enumerate(streams):
+        for spot, edge in ((f, 0), (nf, nf - 1)):
+
+            @pl.when(f == edge)
+            def _():
+                got[spot] = jnp.zeros(got.shape[1:], bf)
+
+            @pl.when(f != edge)
+            def _():
+                with scope("wait_own"):
+                    rs_wait(a, spot)
 
     def middle(l, carry):
         here = at(l)
         gate = own[here, :units] + pre_r[f, here, :units].astype(f32) + pre_r[nf, here, :units].astype(f32)
         up = own[here, units : 2 * units] + pre_r[f, here, units:].astype(f32) + pre_r[nf, here, units:].astype(f32)
-        proj = own[here, 2 * units :]
-        for d in range(1, nf):
-            proj += prj_r[f_at(d), here, :].astype(f32)
+        proj = own[here, 2 * units :] + prj_r[f, here, :].astype(f32) + prj_r[nf, here, :].astype(f32)
         zero, one = choose(f, (l * span).astype(f32), span)
         scale = jnp.sum(
             jnp.where(zero, codes(f, 2), 0.0) + jnp.where(one, codes(f, 3), 0.0), axis=1, keepdims=True
@@ -683,8 +670,8 @@
         def _():
             for a in range(2):
                 z_whole(a, g).wait_send()
-            rs_copy(g, 1).wait_send()
-            prj_copy(g).wait_send()
+            for a in range(2):
+                rs_copy(a, g, 1).wait_send()
 
     for g in range(nf):
 
@@ -759,7 +746,7 @@
         vm(nf, slots, 2 * units),
         vm(nf, slots, units),
         vm(nf + 1, slots, 2 * units),
-        vm(nf, slots, units),
+        vm(nf + 1, slots, units),
         vm(slots, 3 * units, kind=f32),
         vm(local, nf * span, 3 * units),
         vm(nf, slots, depth),

time: 152 us -> 149 us (0.980)
  Pallas kernels: 144 us -> 140 us
    pallas_call x1, Pallas kernels: 144 us -> 140 us  [per_device(): pl.pallas_call(functools.partial(kernel, sizes), out_shape=(jax.ShapeDtyp...]
where the time goes in v9:
time: 149 us; the launch traced here: 148 us
  Pallas kernels  140 us (94%)
  other arithmetic  4.85 us (3%)
  local copies, waits for them, and re-layouts  2.81 us (2%)
    pallas_call x1, Pallas kernels, per_device(): pl.pallas_call(functools.partial(kernel, sizes), out_shape=(jax.ShapeDtyp...  140 us
    sub x1, other arithmetic, adam_update(): new_params = params - learn_rate * (stepped + weight_decay * params)  4.85 us

profile of v9, /device:TPU:0, one launch (start us, length us, event | category | flops | bytes accessed | tf_op | source)
XLA Modules:
  0.0 148.3 jit_solution(5987238064315777215)
XLA Ops:
  0.6 0.0 copy-start
  0.6 0.7 copy-done
  1.3 0.0 copy-start.1
  1.3 0.7 copy-done.1
  2.0 140.0 %shard_map.110 = (bf16[128,4096]{1,0:T(8,128)(2,1)S(1)}, bf16[2,128]{1,0:T(2,128)(2,1)S(1)}, f32[3,4,256,256]{3,2,1,0:T(8,128)S(1)}, f32[3,4,256,256]{3,2,1,0:T(...) custom-call(s32[2,128]{1,0:T(2,128)S(1)} %bitcast.3, bf16[2,128]{1,0:T(2,128)(2,1)S(1)} %bitcast.4, ...), custom_call_target="tpu_custom_call" | custom-call | tf_op jit(solution)/shard_map/pallas_call | solution.py:782
  142.0 4.9 %multiply_subtract_fusion = (f32[3,4,256,256]{3,2,1,0:T(8,128)}, f32[3,4,256,256]{3,2,1,0:T(8,128)}, f32[3,4,256,256]{3,2,1,0:T(8,128)}) fusion(f32[3,4,256,256]{3,2,1,0:T(8,128)S(1)} %get-tuple-element.13, f32[3,4,256,256]{3,2,1,0:T(8,128)S(1)} %get-tuple-element.15, f32[3,4,256,256]{3,2,1,0:T(8,128)S(1)} %get-tuple-element.14, ...), kind=kLoop, calls=%fused_computation.2 | loop fusion | flops 11796480 | bytes 22020096 | tf_op jit(solution)/shard_map/sub | solution.py:29
  146.9 1.0 copy.14
  147.8 0.5 copy.15
Async XLA Ops:
  0.6 0.7 copy-start
  1.3 0.7 copy-start.1
